TPU v7x, 128 devices: a whole 4x4x4 slice. The times are simulated.
128 devices in a mesh: dp: 16 (over z, x), cent: 8 (over y, core).
Axes of the slice: x: 4, y: 4, z: 4, core: 2. Of those that a mesh axis runs over, the one named last changes fastest.
Arguments:
- points: float32 [32768, 512], P('dp'), may hold values from -30 to 30
- centroids: float32 [32768, 512], P('cent'), may hold values from -5 to 5
Outputs:
- new_centroids: float32 [32768, 512], P('cent')
All inputs are finite; a program needn't handle non-finite values.
Results may differ from a plain program's by a relative error of at most 0.0061.
Values sent between devices are 32-bit elements; how exact they have to be, the bound alone decides.
A program may use at most 128 MiB of HBM per device.

v0:
```python
import jax
import jax.numpy as jnp
from jax import lax
from jax.sharding import PartitionSpec as P

D = 512


def from_everyone(value, axis):
    length = lax.axis_size(axis)
    return lax.all_to_all(
        jnp.broadcast_to(value[None], (length, *value.shape)), axis, 0, 0, tiled=True
    )


def collected_together(value, axis):
    leaves = jax.tree.leaves(value)
    turns = sorted(range(len(leaves)), key=lambda k: -leaves[k].size)
    width = (1, *leaves[turns[0]].shape)[-1]
    lines = [
        jnp.pad(leaves[k].reshape(-1), (0, -leaves[k].size % width)).reshape(-1, width)
        for k in turns
    ]
    both, at, found = (from_everyone(jnp.concatenate(lines), axis), 0, {})
    for k, line in zip(turns, lines):
        piece = both[:, at : at + len(line)].reshape(len(both), -1)
        found[k] = piece[:, : leaves[k].size].reshape(-1, *leaves[k].shape)
        at += len(line)
    numbers = iter(range(len(leaves)))
    return jax.tree.map(lambda _: found[next(numbers)], value)


def folded_in_pairs(pieces, combine):
    while len(jax.tree.leaves(pieces)[0]) > 1:
        pieces = jax.vmap(combine)(
            *(jax.tree.map(lambda part: part[side::2], pieces) for side in (0, 1))
        )
    return jax.tree.map(lambda part: part[0], pieces)


def combined_all(value, axis, combine):
    pieces = collected_together(value, axis)
    return folded_in_pairs(pieces, combine)


def join_stats(first, second):
    high = jnp.maximum(first[0], second[0])
    summed = first[1] * jnp.exp(first[0] - high) + second[1] * jnp.exp(second[0] - high)
    return (high, summed)


def body(points, centroids):
    point_half = points.astype(jnp.bfloat16)
    cent_half = centroids.astype(jnp.bfloat16)
    sq_norm = jnp.sum(centroids * centroids, axis=1)
    scale = 1.0 / jnp.sqrt(jnp.float32(D))
    inner = lax.dot_general(
        point_half, cent_half, (((1,), (1,)), ((), ())), preferred_element_type=jnp.float32
    )
    logit = (2.0 * inner - sq_norm[None, :]) * scale
    local_top = jnp.max(logit, axis=1)
    local_expo = jnp.exp(logit - local_top[:, None])
    local_total = jnp.sum(local_expo, axis=1)
    top, total = combined_all((local_top, local_total), "cent", join_stats)
    expo = local_expo * jnp.exp(local_top - top)[:, None]
    resp = (expo / total[:, None]).astype(jnp.bfloat16)
    weighted = lax.dot_general(
        resp, point_half, (((0,), (0,)), ((), ())), preferred_element_type=jnp.float32
    )
    counts = jnp.sum(resp, axis=0, dtype=jnp.float32)
    summed, counted = lax.psum((weighted, counts), "dp")
    return (summed + centroids) / (counted + 1.0)[:, None]


def solution(mesh):
    placed = (P("dp", None), P("cent", None))
    return jax.shard_map(
        body, mesh=mesh, in_specs=placed, out_specs=P("cent", None), check_vma=False
    )
```

profile of v0, /device:TPU:0, one launch (start us, length us, event | category | flops | bytes accessed | tf_op | source)
XLA Modules:
  0.0 247.4 jit_solution(671301946056418441)
XLA Ops:
  6.5 0.0 all-reduce.2.cloned.1.call-start
  6.5 4.0 %multiply_reduce_fusion = f32[4096]{0:T(1024)S(1)} fusion(f32[4096,512]{1,0:T(8,128)} %param.3), kind=kLoop, calls=%fused_computation.7 | loop fusion | flops 4190208 | bytes 8404992 | tf_op jit(solution)/shard_map/reduce_sum | solution.py:55
  10.5 19.2 %fusion.1 = (f32[2048]{0:T(1024)S(1)}, f32[2048,4096]{1,0:T(8,128)}) fusion(f32[4096]{0:T(1024)S(1)} %multiply_reduce_fusion, f32[4096,512]{1,0:T(8,128)} %param.3, f32[2048,512]{1,0:T(8,128)} %param.2), kind=kOutput, calls=%fused_computation.5 | convolution fusion | flops 8626632704 | bytes 46161920 | tf_op jit(solution)/shard_map/dot_general | solution.py:57
  29.8 15.1 %fusion = f32[2048]{0:T(1024)S(1)} fusion(f32[2048,4096]{1,0:T(8,128)} %get-tuple-element.16, f32[2048]{0:T(1024)S(1)} %get-tuple-element.15, f32[4096]{0:T(1024)S(1)} %multiply_reduce_fusion), kind=kLoop, calls=%fused_computation.4 | loop fusion | flops 41940992 | bytes 33587200 | tf_op jit(solution)/shard_map/reduce_sum | solution.py:63
  44.9 10.5 %all_to_all.5 = f32[8,2,2048]{2,1,0:T(2,128)S(1)} all-to-all(f32[8,2,2048]{2,1,0:T(2,128)S(1)} %broadcast_in_dim.2), channel_id=1, replica_groups=mesh['dp'=16,'cent'=8] {'cent'}, dimensions={0} | all-to-all | bytes 262144 | tf_op jit(solution)/shard_map/all_to_all | solution.py:11
  55.4 0.1 fusion.8
  55.9 17.1 %convert_reduce_fusion = (f32[4096]{0:T(1024)S(1)}, bf16[2048,4096]{1,0:T(8,128)(2,1)S(1)}) fusion(f32[2048]{0:T(1024)S(1)} %bitcast.12, f32[2048]{0:T(1024)S(1)} %subtract_exponential_fusion.1, f32[2048]{0:T(1024)S(1)} %get-tuple-element.15, f32[4096]{0:T(1024)S(1)} %multiply_reduce_fusion, f32[2048,4096]{1,0:T(8,128)} %get-tuple-element.16), kind=kLoop, calls=%fused_computation | loop fusion | flops 75493376 | bytes 50388992 | tf_op jit(solution)/shard_map/reduce_sum | solution.py:70
  73.1 14.5 %fusion.4 = f32[4096,512]{1,0:T(8,128)} fusion(bf16[2048,4096]{1,0:T(8,128)(2,1)S(1)} %get-tuple-element.6, f32[2048,512]{1,0:T(8,128)} %param.2), kind=kOutput, calls=%fused_computation.10 | convolution fusion | flops 8590983168 | bytes 29360128 | tf_op jit(solution)/shard_map/dot_general | solution.py:67
  87.5 0.0 all-reduce.2.cloned.1.call-update
  87.6 77.2 %psum.15 = f32[4096]{0:T(1024)S(1)} all-reduce(f32[4096]{0:T(1024)S(1)} %get-tuple-element.5), channel_id=1, replica_groups=mesh['dp'=16,'cent'=8] {'dp'}, use_global_device_ids=true, to_apply=%region_5.6 | all-reduce | flops 4096 | bytes 32768 | tf_op jit(solution)/shard_map/psum | solution.py:71
  164.7 65.9 %all-reduce.2.cloned.1.call-done = f32[4096,512]{1,0:T(8,128)} async-done(((f32[4096,512]{1,0:T(8,128)}), f32[4096,512]{1,0:T(8,128)}) %all-reduce.2.cloned.1.call-update) | async-done | bytes 8388624 | tf_op jit(solution)/shard_map/psum | solution.py:71
  230.7 9.9 %add_divide_fusion = f32[4096,512]{1,0:T(8,128)} fusion(f32[4096,512]{1,0:T(8,128)} %all-reduce.2.cloned.1.call-done, f32[4096,512]{1,0:T(8,128)} %param.3, f32[4096]{0:T(1024)S(1)} %broadcast_add_fusion), kind=kLoop, calls=%fused_computation.6 | loop fusion | flops 4194304 | bytes 25182208 | tf_op jit(solution)/shard_map/div | solution.py:72
  (16 shorter events, 0.5 us)
Async XLA Ops:
  6.5 224.1 %all-reduce.2.cloned.1.call-start = ((), (), s32[]{:S(2)}) async-start(), calls=%async_computation.1 | async-start | bytes 16777216 | tf_op jit(solution)/shard_map/psum | solution.py:71
Sparse Core Ops, SparseCore 0:
  87.7 142.9 all-reduce.1
where the time goes:
time: 248 us; the launch traced here: 247 us
  blocking collectives  87.6 us (35%)
  waiting for transfers between devices  66 us (27%)
  other arithmetic  46.2 us (19%)
  matrix products  33.7 us (14%)
  between operations  13.5 us (5%)
    psum x1, blocking collectives, body(): summed, counted = lax.psum((weighted, counts), 'dp')  77.2 us
    psum x1, waiting for transfers between devices, body(): summed, counted = lax.psum((weighted, counts), 'dp')  65.9 us
    dot_general x1, matrix products, body(): lax.dot_general(point_half, cent_half, (((1,), (1,)), ((), ())), preferre...  19.2 us
    reduce_sum x1, other arithmetic, body(): counts = jnp.sum(resp, axis=0, dtype=jnp.float32)  17.1 us
    reduce_sum x1, other arithmetic, body(): local_total = jnp.sum(local_expo, axis=1)  15.1 us
    dot_general x1, matrix products, body(): lax.dot_general(resp, point_half, (((0,), (0,)), ((), ())), preferred_ele...  14.5 us
    all_to_all x1, blocking collectives, from_everyone(): lax.all_to_all(jnp.broadcast_to(value[None], (length, *value.shape)), axi...  10.5 us
    div x1, other arithmetic, body(): return (summed + centroids) / (counted + 1.0)[:, None]  9.9 us
  transfers between devices with their start and end apart: 1, of which 1 were waited for; matrix products, arithmetic and copies ran while one was open for 0% of the time, Pallas kernels for 0%

commit v1 on v0

v1 whole, which is shorter than its diff:
```python
import functools

import jax
import jax.numpy as jnp
from jax import lax
from jax.experimental import pallas as pl
from jax.experimental.pallas import tpu as pltpu
from jax.sharding import PartitionSpec as P

MESH = pl.DeviceIdType.MESH
F32, BF16 = jnp.float32, jnp.bfloat16
LOG2E = 1.4426950408889634


def kernel(
    n_cent,
    points,
    cents,
    out,
    ph,
    pstage,
    cstage,
    ch,
    sqb,
    logit0,
    logit1,
    expo,
    mtop,
    msum,
    factor,
    stat,
    statr,
    row,
    w,
    got,
    r1,
    r2,
    t1,
    t2,
    cfin,
    cnt,
    cntx,
    cntz,
    ssem,
    rsem,
    lsem,
):
    n_points, width = ph.shape
    chunk = ch.shape[0]
    n_chunk = mtop.shape[0]
    tile = logit0.shape[1]
    n_tile = n_points // tile
    rows = w.shape[4]
    scale = LOG2E / width**0.5

    dp = lax.axis_index("dp")
    ce = lax.axis_index("cent")
    x, z = lax.rem(dp, 4), lax.div(dp, 4)

    def at_x(d):
        return (z * 4 + lax.rem(x + d, 4), ce)

    def at_z(d):
        return (lax.rem(z + d, 4) * 4 + x, ce)

    def at_cent(d):
        return (dp, lax.rem(ce + d, n_cent))

    peers = [at_x(d) for d in (1, 2, 3)] + [at_z(d) for d in (1, 2, 3)]
    peers += [at_cent(d) for d in range(1, n_cent)]
    barrier = pltpu.get_barrier_semaphore()
    for peer in peers:
        pl.semaphore_signal(barrier, inc=1, device_id=peer, device_id_type=MESH)

    used = [0]
    sent = []

    def send(src, dst, dev):
        i = used[0]
        used[0] += 1
        copy = pltpu.make_async_remote_copy(
            src_ref=src,
            dst_ref=dst,
            send_sem=ssem.at[i],
            recv_sem=rsem.at[i],
            device_id=dev,
            device_id_type=MESH,
        )
        copy.start()
        sent.append(copy)
        return copy

    part = n_points // 4

    def load_points(i):
        return pltpu.make_async_copy(
            points.at[pl.ds(i * part, part)], pstage.at[i % 2], lsem.at[i % 2]
        )

    def load_cents(i, slot):
        return pltpu.make_async_copy(
            cents.at[pl.ds(i * chunk, chunk)], cstage.at[slot], lsem.at[2 + slot]
        )

    load_points(0).start()
    load_points(1).start()
    load_cents(0, 0).start()
    load_cents(1, 1).start()
    for i in range(4):
        load_points(i).wait()
        ph[pl.ds(i * part, part), :] = pstage[i % 2].astype(BF16)
        if i + 2 < 4:
            load_points(i + 2).start()

    def first(t, logit):
        at = pl.multiple_of(t * tile, tile)
        inner = lax.dot_general(
            ch[...], ph[pl.ds(at, tile), :], (((1,), (1,)), ((), ())),
            preferred_element_type=F32,
        )
        value = inner * (2.0 * scale) - jnp.concatenate([sqb[...]] * (tile // 128), axis=1)
        logit[...] = value
        return jnp.max(value, axis=0, keepdims=True)

    def second(c, t, logit, high):
        at = pl.multiple_of(t * tile, tile)
        e = jnp.exp2(logit[...] - high)
        base = pl.multiple_of(c * chunk, chunk)
        expo[pl.ds(base, chunk), pl.ds(at, tile)] = e.astype(BF16)
        mtop[c, :, pl.ds(at, tile)] = high
        msum[c, :, pl.ds(at, tile)] = jnp.sum(e, axis=0, keepdims=True)

    def on_chunk(c, carry):
        slot = lax.rem(c, 2)
        load_cents(c, slot).wait()
        value = cstage[slot]
        ch[...] = value.astype(BF16)
        sqb[...] = jnp.broadcast_to(
            jnp.sum(value * value, axis=1, keepdims=True) * scale, sqb.shape
        )

        @pl.when(c + 2 < n_chunk)
        def _():
            load_cents(c + 2, slot).start()

        high = first(0, logit0)

        def pair(j, high):
            other = first(2 * j + 1, logit1)
            second(c, 2 * j, logit0, high)
            high = first(lax.rem(2 * j + 2, n_tile), logit0)
            second(c, 2 * j + 1, logit1, other)
            return high

        lax.fori_loop(0, n_tile // 2, pair, high)
        return carry

    lax.fori_loop(0, n_chunk, on_chunk, 0)

    top = functools.reduce(jnp.maximum, [mtop[c] for c in range(n_chunk)])
    total = sum(msum[c] * jnp.exp2(mtop[c] - top) for c in range(n_chunk))
    for i in range(n_points // 128):
        stat[0, i : i + 1, :] = top[:, i * 128 : (i + 1) * 128]
        stat[1, i : i + 1, :] = total[:, i * 128 : (i + 1) * 128]
    pl.semaphore_wait(barrier, len(peers))
    copies = [send(stat, statr.at[d - 1], at_cent(d)) for d in range(1, n_cent)]

    us, vs = (x, z), (z, x)
    fins = []
    for c in range(2):
        for h in range(2):
            at = ((c * 4 + us[c]) * 2 + h) * (4 * rows) + vs[c] * rows
            fins.append(
                pltpu.make_async_copy(
                    cents.at[pl.ds(pl.multiple_of(at, rows), rows)],
                    cfin.at[c, h],
                    lsem.at[4 + 2 * c + h],
                )
            )
            fins[-1].start()

    for copy in copies:
        copy.wait_recv()
    tops = [stat[0]] + [statr[d, 0] for d in range(n_cent - 1)]
    sums = [stat[1]] + [statr[d, 1] for d in range(n_cent - 1)]
    high = functools.reduce(jnp.maximum, tops)
    inverse = 1.0 / sum(s * jnp.exp2(t - high) for t, s in zip(tops, sums))
    for i in range(n_points // 128):
        row[0, :, i * 128 : (i + 1) * 128] = high[i : i + 1, :]
        row[1, :, i * 128 : (i + 1) * 128] = inverse[i : i + 1, :]
    for c in range(n_chunk):
        factor[c] = jnp.exp2(mtop[c] - row[0]) * row[1]

    def produce(c, bu, h):
        block = (c * 4 + bu) * 2 + h
        at = pl.multiple_of(block * (4 * rows), 4 * rows)
        group = lax.div(block * (4 * rows), chunk)
        acc = jnp.zeros((4 * rows, width), F32)
        count = jnp.zeros((4 * rows, 128), F32)
        step = n_points // 4
        for k in range(4):
            cols = slice(k * step, (k + 1) * step)
            resp = (expo[pl.ds(at, 4 * rows), cols].astype(F32) * factor[group, :, cols]).astype(BF16)
            acc += jnp.dot(resp, ph[cols, :], preferred_element_type=F32)
            wide = resp.astype(F32)
            for l in range(step // 128):
                count += wide[:, l * 128 : (l + 1) * 128]
        w[c, bu, h] = acc.reshape(4, rows, width)
        line = jnp.sum(count.T, axis=0, keepdims=True)
        for b in range(4):
            cnt[block, b, :, :rows] = line[:, b * rows : (b + 1) * rows]

    ups = (at_x(1), at_z(1))
    downs = (at_x(3), at_z(3))
    u = [[lax.rem(us[c] + d, 4) for d in range(4)] for c in range(2)]
    v = [[lax.rem(vs[c] + d, 4) for d in range(4)] for c in range(2)]
    order = (2, 1, 3, 0)

    a_up, a_dn, b_up, b_dn = {}, {}, {}, {}
    for c in range(2):
        produce(c, u[c][2], 0)
        for d in order:
            b = v[c][d]
            a_up[c, d] = send(w.at[c, u[c][2], 0, b], r1.at[c, 0, b], ups[c])
        produce(c, u[c][2], 1)
        for d in order:
            b = v[c][d]
            a_dn[c, d] = send(w.at[c, u[c][2], 1, b], r1.at[c, 1, b], downs[c])
    own = []
    for c in range(2):
        produce(c, u[c][1], 1)
        own.append(send(w.at[c, u[c][1], 1], r2.at[c, 0, 1], ups[c]))
        produce(c, u[c][3], 0)
        own.append(send(w.at[c, u[c][3], 0], r2.at[c, 1, 0], downs[c]))
    for c in range(2):
        produce(c, u[c][1], 0)
        produce(c, u[c][3], 1)
    for c in range(2):
        produce(c, u[c][0], 0)
        produce(c, u[c][0], 1)
    copies = [send(cnt, cntx.at[d - 1], at_x(d)) for d in (1, 2, 3)]

    for d in order:
        for c in range(2):
            b = v[c][d]
            a_up[c, d].wait_recv()
            w[c, u[c][1], 0, b] += r1[c, 0, b]
            b_up[c, d] = send(w.at[c, u[c][1], 0, b], r2.at[c, 0, 0, b], ups[c])
            a_dn[c, d].wait_recv()
            w[c, u[c][3], 1, b] += r1[c, 1, b]
            b_dn[c, d] = send(w.at[c, u[c][3], 1, b], r2.at[c, 1, 1, b], downs[c])
    for copy in copies:
        copy.wait_recv()
    for copy in copies:
        copy.wait_send()
    sent[:] = [copy for copy in sent if all(copy is not done for done in copies)]
    cnt[...] = cnt[...] + cntx[0] + cntx[1] + cntx[2]
    copies = [send(cnt, cntz.at[d - 1], at_z(d)) for d in (1, 2, 3)]
    for copy in own:
        copy.wait_recv()

    ups2, downs2 = ups[::-1], downs[::-1]
    s_up, s_dn, q = {}, {}, []
    for d in order:
        for c in range(2):
            b, me = v[c][d], us[c]
            b_up[c, d].wait_recv()
            b_dn[c, d].wait_recv()
            for h in range(2):
                w[c, me, h, b] += r2[c, 0, h, b] + r2[c, 1, h, b]
            if d == 2:
                s_up[c] = send(w.at[c, me, 0, b], t1.at[c, 0], ups2[c])
                s_dn[c] = send(w.at[c, me, 1, b], t1.at[c, 1], downs2[c])
            if d == 1:
                q.append(send(w.at[c, me, 1, b], t2.at[c, 0, 1], ups2[c]))
            if d == 3:
                q.append(send(w.at[c, me, 0, b], t2.at[c, 1, 0], downs2[c]))
    for c in range(2):
        me = us[c]
        s_up[c].wait_recv()
        w[c, me, 0, v[c][1]] += t1[c, 0]
        q.append(send(w.at[c, me, 0, v[c][1]], t2.at[c, 0, 0], ups2[c]))
        s_dn[c].wait_recv()
        w[c, me, 1, v[c][3]] += t1[c, 1]
        q.append(send(w.at[c, me, 1, v[c][3]], t2.at[c, 1, 1], downs2[c]))
    for copy in copies + q:
        copy.wait_recv()
    for copy in fins:
        copy.wait()

    g_up, g_dn = {}, {}
    for c in range(2):
        me, b = us[c], vs[c]
        for h in range(2):
            block = (c * 4 + me) * 2 + h
            line = cnt[block, b] + cntz[0, block, b] + cntz[1, block, b] + cntz[2, block, b]
            count = jnp.broadcast_to(line, (128, 128)).T[:rows]
            count = jnp.concatenate([count] * (width // 128), axis=1)
            value = w[c, me, h, b] + t2[c, 0, h] + t2[c, 1, h]
            got[c, me, h, b] = (value + cfin[c, h]) / (count + 1.0)
        mine = got.at[c, me, :, b]
        g_up[c] = send(mine, mine, ups2[c])
        g_dn[c] = send(mine, mine, downs2[c])

    h_up, h_dn, f_up, f_dn = {}, {}, {}, {}

    def spread(c, d):
        piece = got.at[c, us[c], :, v[c][d]]
        h_up[c, d] = send(piece, piece, ups[c])
        h_dn[c, d] = send(piece, piece, downs[c])

    def save(piece_of):
        pltpu.make_async_copy(piece_of(got), piece_of(out), lsem.at[8]).start()

    for c in range(2):
        spread(c, 0)
        save(lambda ref: ref.at[c, us[c], :, vs[c]])
    for c in range(2):
        me = us[c]
        g_up[c].wait_recv()
        piece = got.at[c, me, 0, v[c][3]]
        f_up[c] = send(piece, piece, ups2[c])
        spread(c, 3)
        save(lambda ref: ref.at[c, me, :, v[c][3]])
        g_dn[c].wait_recv()
        piece = got.at[c, me, 1, v[c][1]]
        f_dn[c] = send(piece, piece, downs2[c])
        spread(c, 1)
        save(lambda ref: ref.at[c, me, :, v[c][1]])
    k_up, k_dn = {}, {}

    def onward(c, d):
        b = v[c][d]
        h_up[c, d].wait_recv()
        piece = got.at[c, u[c][3], 0, b]
        k_up[c, d] = send(piece, piece, ups[c])
        save(lambda ref: ref.at[c, u[c][3], :, b])
        h_dn[c, d].wait_recv()
        piece = got.at[c, u[c][1], 1, b]
        k_dn[c, d] = send(piece, piece, downs[c])
        save(lambda ref: ref.at[c, u[c][1], :, b])

    for c in range(2):
        onward(c, 0)
    for c in range(2):
        f_up[c].wait_recv()
        f_dn[c].wait_recv()
        spread(c, 2)
        save(lambda ref: ref.at[c, us[c], :, v[c][2]])
    for d in (3, 1, 2):
        for c in range(2):
            onward(c, d)
    for d in (0, 3, 1, 2):
        for c in range(2):
            k_up[c, d].wait_recv()
            k_dn[c, d].wait_recv()
            save(lambda ref: ref.at[c, u[c][2], :, v[c][d]])
    for copy in sent:
        copy.wait_send()
    pltpu.make_async_copy(got, out, lsem.at[8]).wait()


def body(points, centroids):
    n_points, width = points.shape
    n_rows = centroids.shape[0]
    n_cent = lax.axis_size("cent")
    chunk, tile = n_rows // 4, 512
    rows = n_rows // 64
    pieces = (2, 4, 2, 4, rows, width)
    n_copies = 2 * 44 + (n_cent - 1) + 6
    vm = pltpu.VMEM
    flat = (n_rows // chunk, 1, n_points)
    scratch = [
        vm((n_points, width), BF16),
        vm((2, n_points // 4, width), F32),
        vm((2, chunk, width), F32),
        vm((chunk, width), BF16),
        vm((chunk, 128), F32),
        vm((chunk, tile), F32),
        vm((chunk, tile), F32),
        vm((n_rows, n_points), BF16),
        vm(flat, F32),
        vm(flat, F32),
        vm(flat, F32),
        vm((2, n_points // 128, 128), F32),
        vm((n_cent - 1, 2, n_points // 128, 128), F32),
        vm((2, 1, n_points), F32),
        vm(pieces, F32),
        vm(pieces, F32),
        vm((2, 2, 4, rows, width), F32),
        vm((2, 2, 2, 4, rows, width), F32),
        vm((2, 2, rows, width), F32),
        vm((2, 2, 2, rows, width), F32),
        vm((2, 2, rows, width), F32),
        vm((16, 4, 1, 128), F32),
        vm((3, 16, 4, 1, 128), F32),
        vm((3, 16, 4, 1, 128), F32),
        pltpu.SemaphoreType.DMA((n_copies,)),
        pltpu.SemaphoreType.DMA((n_copies,)),
        pltpu.SemaphoreType.DMA((9,)),
    ]
    result = pl.pallas_call(
        functools.partial(kernel, n_cent),
        out_shape=jax.ShapeDtypeStruct(pieces, F32),
        in_specs=[pl.BlockSpec(memory_space=pl.ANY)] * 2,
        out_specs=pl.BlockSpec(memory_space=pl.ANY),
        scratch_shapes=scratch,
        compiler_params=pltpu.CompilerParams(
            collective_id=0, has_side_effects=True, vmem_limit_bytes=67_000_000
        ),
    )(points, centroids)
    return result.reshape(n_rows, width)


def solution(mesh):
    placed = (P("dp", None), P("cent", None))
    return jax.shard_map(
        body, mesh=mesh, in_specs=placed, out_specs=P("cent", None), check_vma=False
    )
```

time: 248 us -> 133 us (0.54)
  Pallas kernels: 0 us -> 125 us
  blocking collectives: 87.6 us -> 0 us
  waiting for transfers between devices: 66 us -> 0 us
  other arithmetic: 46.2 us -> 0 us
  matrix products: 33.7 us -> 0 us
  between operations: 13.5 us -> 0.01 us
  local copies, waits for them, and re-layouts: 0.42 us -> 7.76 us
    pallas_call x0 -> x1, Pallas kernels: none -> 125 us  [body(): pl.pallas_call(functools.partial(kernel, n_cent), out_shape=jax.ShapeDtyp...]
    psum x1 -> x0, blocking collectives: 77.2 us -> none  [body(): summed, counted = lax.psum((weighted, counts), 'dp')]
    psum x1 -> x0, waiting for transfers between devices: 65.9 us -> none  [body(): summed, counted = lax.psum((weighted, counts), 'dp')]
    reduce_sum x3 -> x0, other arithmetic: 36.2 us -> none  [the longest x1 17.1 us: body(): counts = jnp.sum(resp, axis=0, dtype=jnp.float32)]
    dot_general x2 -> x0, matrix products: 33.7 us -> none  [the longest x1 19.2 us: body(): lax.dot_general(point_half, cent_half, (((1,), (1,)), ((), ())), preferre...]
    all_to_all x1 -> x0, blocking collectives: 10.5 us -> none  [from_everyone(): lax.all_to_all(jnp.broadcast_to(value[None], (length, *value.shape)), axi...]
    div x1 -> x0, other arithmetic: 9.9 us -> none  [body(): return (summed + centroids) / (counted + 1.0)[:, None]]
    unnamed x0 -> x1, local copies, waits for them, and re-layouts: none -> 7.76 us
  transfers between devices with their start and end apart: 1 -> 0, of which waited for: 1 -> 0; matrix products, arithmetic and copies ran while one was open for 0% -> 0% of each run, Pallas kernels for 0% -> 0%
where the time goes in v1:
time: 133 us
  Pallas kernels  125 us (94%)
  local copies, waits for them, and re-layouts  7.76 us (6%)
    pallas_call x1, Pallas kernels, body(): pl.pallas_call(functools.partial(kernel, n_cent), out_shape=jax.ShapeDtyp...  125 us
    unnamed x1, local copies, waits for them, and re-layouts  7.76 us

profile of v1, /device:TPU:0, one launch (start us, length us, event | category | flops | bytes accessed | tf_op | source)
XLA Modules:
  0.0 132.6 jit_solution(5414291800983831756)
XLA Ops:
  0.0 124.9 %shard_map.28 = f32[2,4,2,4,64,512]{5,4,3,2,1,0:T(8,128)} custom-call(f32[2048,512]{1,0:T(8,128)} %points.1, f32[4096,512]{1,0:T(8,128)} %cents.1), custom_call_target="tpu_custom_call" | custom-call | tf_op jit(solution)/shard_map/pallas_call | solution.py:402
  124.9 7.8 %copy.4 = f32[4096,512]{1,0:T(8,128)} copy(f32[4096,512]{1,0:T(8,128)} %bitcast.1) | data formatting | bytes 16777216

commit v2 on v1

--- a/solution.py
+++ b/solution.py
@@ -16,9 +16,8 @@
     n_cent,
     points,
     cents,
-    out,
+    got,
     ph,
-    pstage,
     cstage,
     ch,
     sqb,
@@ -32,7 +31,6 @@
     statr,
     row,
     w,
-    got,
     r1,
     r2,
     t1,
@@ -46,7 +44,7 @@
     lsem,
 ):
     n_points, width = ph.shape
-    chunk = ch.shape[0]
+    chunk = ch.shape[1]
     n_chunk = mtop.shape[0]
     tile = logit0.shape[1]
     n_tile = n_points // tile
@@ -75,10 +73,12 @@
     used = [0]
     sent = []
 
-    def send(src, dst, dev):
-        i = used[0]
-        used[0] += 1
-        copy = pltpu.make_async_remote_copy(
+    def slots(n):
+        used[0] += n
+        return used[0] - n
+
+    def remote(i, src, dst, dev):
+        return pltpu.make_async_remote_copy(
             src_ref=src,
             dst_ref=dst,
             send_sem=ssem.at[i],
@@ -86,6 +86,9 @@
             device_id=dev,
             device_id_type=MESH,
         )
+
+    def send(src, dst, dev):
+        copy = remote(slots(1), src, dst, dev)
         copy.start()
         sent.append(copy)
         return copy
@@ -94,68 +97,77 @@
 
     def load_points(i):
         return pltpu.make_async_copy(
-            points.at[pl.ds(i * part, part)], pstage.at[i % 2], lsem.at[i % 2]
-        )
-
-    def load_cents(i, slot):
+            points.at[i], w.at[0, i], lsem.at[i]
+        )
+
+    def load_cents(i):
+        slot = lax.rem(i, 2)
         return pltpu.make_async_copy(
-            cents.at[pl.ds(i * chunk, chunk)], cstage.at[slot], lsem.at[2 + slot]
+            cents.at[pl.ds(i * chunk, chunk)], cstage.at[slot], lsem.at[4 + slot]
         )
 
     load_points(0).start()
-    load_points(1).start()
-    load_cents(0, 0).start()
-    load_cents(1, 1).start()
+    load_cents(0).start()
+    for i in range(1, 4):
+        load_points(i).start()
+    load_cents(1).start()
+
+    def round_cents(i):
+        slot = lax.rem(i, 2)
+        value = cstage[slot]
+        ch[slot] = value.astype(BF16)
+        sqb[slot] = jnp.broadcast_to(
+            jnp.sum(value * value, axis=1, keepdims=True) * scale, (chunk, 128)
+        )
+
+    def first(c, t, logit):
+        slot = lax.rem(c, 2)
+        inner = lax.dot_general(
+            ch[slot], ph[t * tile : (t + 1) * tile, :], (((1,), (1,)), ((), ())),
+            preferred_element_type=F32,
+        )
+        value = inner * (2.0 * scale) - jnp.concatenate([sqb[slot]] * (tile // 128), axis=1)
+        logit[...] = value
+        return jnp.max(value, axis=0, keepdims=True)
+
+    def second(c, t, logit, high):
+        at = slice(t * tile, (t + 1) * tile)
+        e = jnp.exp2(logit[...] - high)
+        base = pl.multiple_of(c * chunk, chunk)
+        expo[pl.ds(base, chunk), at] = e.astype(BF16)
+        mtop[c, :, at] = high
+        msum[c, :, at] = jnp.sum(e, axis=0, keepdims=True)
+
+    logits = (logit0, logit1)
+
+    def on_chunk(c, high, last):
+        if not last:
+            load_cents(c + 1).wait()
+
+            @pl.when(c + 2 < n_chunk)
+            def _():
+                load_cents(c + 2).start()
+
+        for t in range(n_tile):
+            if t + 1 < n_tile:
+                after = first(c, t + 1, logits[(t + 1) % 2])
+                if t == 0 and not last:
+                    round_cents(c + 1)
+            elif not last:
+                after = first(c + 1, 0, logits[(t + 1) % 2])
+            second(c, t, logits[t % 2], high)
+            high = after
+        return high
+
     for i in range(4):
         load_points(i).wait()
-        ph[pl.ds(i * part, part), :] = pstage[i % 2].astype(BF16)
-        if i + 2 < 4:
-            load_points(i + 2).start()
-
-    def first(t, logit):
-        at = pl.multiple_of(t * tile, tile)
-        inner = lax.dot_general(
-            ch[...], ph[pl.ds(at, tile), :], (((1,), (1,)), ((), ())),
-            preferred_element_type=F32,
-        )
-        value = inner * (2.0 * scale) - jnp.concatenate([sqb[...]] * (tile // 128), axis=1)
-        logit[...] = value
-        return jnp.max(value, axis=0, keepdims=True)
-
-    def second(c, t, logit, high):
-        at = pl.multiple_of(t * tile, tile)
-        e = jnp.exp2(logit[...] - high)
-        base = pl.multiple_of(c * chunk, chunk)
-        expo[pl.ds(base, chunk), pl.ds(at, tile)] = e.astype(BF16)
-        mtop[c, :, pl.ds(at, tile)] = high
-        msum[c, :, pl.ds(at, tile)] = jnp.sum(e, axis=0, keepdims=True)
-
-    def on_chunk(c, carry):
-        slot = lax.rem(c, 2)
-        load_cents(c, slot).wait()
-        value = cstage[slot]
-        ch[...] = value.astype(BF16)
-        sqb[...] = jnp.broadcast_to(
-            jnp.sum(value * value, axis=1, keepdims=True) * scale, sqb.shape
-        )
-
-        @pl.when(c + 2 < n_chunk)
-        def _():
-            load_cents(c + 2, slot).start()
-
-        high = first(0, logit0)
-
-        def pair(j, high):
-            other = first(2 * j + 1, logit1)
-            second(c, 2 * j, logit0, high)
-            high = first(lax.rem(2 * j + 2, n_tile), logit0)
-            second(c, 2 * j + 1, logit1, other)
-            return high
-
-        lax.fori_loop(0, n_tile // 2, pair, high)
-        return carry
-
-    lax.fori_loop(0, n_chunk, on_chunk, 0)
+        ph[i * part : (i + 1) * part, :] = w[0, i].reshape(part, width).astype(BF16)
+        if i == 0:
+            load_cents(0).wait()
+            round_cents(0)
+    high = first(0, 0, logit0)
+    high = lax.fori_loop(0, n_chunk - 1, lambda c, high: on_chunk(c, high, False), high)
+    on_chunk(n_chunk - 1, high, True)
 
     top = functools.reduce(jnp.maximum, [mtop[c] for c in range(n_chunk)])
     total = sum(msum[c] * jnp.exp2(mtop[c] - top) for c in range(n_chunk))
@@ -174,7 +186,7 @@
                 pltpu.make_async_copy(
                     cents.at[pl.ds(pl.multiple_of(at, rows), rows)],
                     cfin.at[c, h],
-                    lsem.at[4 + 2 * c + h],
+                    lsem.at[6 + 2 * c + h],
                 )
             )
             fins[-1].start()
@@ -216,28 +228,58 @@
     v = [[lax.rem(vs[c] + d, 4) for d in range(4)] for c in range(2)]
     order = (2, 1, 3, 0)
 
+    def place(c):
+        return x * (1 - c) + z * c, z * (1 - c) + x * c
+
+    def along(c, d):
+        return (lax.rem(z + c * d, 4) * 4 + lax.rem(x + (1 - c) * d, 4), ce)
+
+    far, near = slots(16), slots(4)
+
+    def far_copy(c, h, k):
+        here, other = place(c)
+        b = lax.rem(other + order[k], 4)
+        return remote(
+            far + (c * 2 + h) * 4 + k,
+            w.at[c, lax.rem(here + 2, 4), h, b],
+            r1.at[c, h, b],
+            along(c, 1 + 2 * h),
+        )
+
+    def near_copy(c, h):
+        here, _ = place(c)
+        d = 3 - 2 * h
+        return remote(
+            near + c * 2 + h, w.at[c, lax.rem(here + d, 4), h], r2.at[c, 1 - h, h], along(c, d)
+        )
+
+    def farthest(i, carry):
+        c, h = lax.rem(i, 2), lax.div(i, 2)
+        produce(c, lax.rem(place(c)[0] + 2, 4), h)
+        for k in range(4):
+            far_copy(c, h, k).start()
+        return carry
+
+    def nearest(i, carry):
+        c, h = lax.rem(i, 2), 1 - lax.div(i, 2)
+        produce(c, lax.rem(place(c)[0] + 3 - 2 * h, 4), h)
+        near_copy(c, h).start()
+        return carry
+
+    def others(i, carry):
+        c, h, mine = lax.rem(i, 2), lax.rem(lax.div(i, 2), 2), lax.div(i, 4)
+        produce(c, lax.rem(place(c)[0] + (1 - mine) * (1 + 2 * h), 4), h)
+        return carry
+
+    lax.fori_loop(0, 4, farthest, 0)
+    lax.fori_loop(0, 4, nearest, 0)
+    lax.fori_loop(0, 8, others, 0)
     a_up, a_dn, b_up, b_dn = {}, {}, {}, {}
     for c in range(2):
-        produce(c, u[c][2], 0)
-        for d in order:
-            b = v[c][d]
-            a_up[c, d] = send(w.at[c, u[c][2], 0, b], r1.at[c, 0, b], ups[c])
-        produce(c, u[c][2], 1)
-        for d in order:
-            b = v[c][d]
-            a_dn[c, d] = send(w.at[c, u[c][2], 1, b], r1.at[c, 1, b], downs[c])
-    own = []
-    for c in range(2):
-        produce(c, u[c][1], 1)
-        own.append(send(w.at[c, u[c][1], 1], r2.at[c, 0, 1], ups[c]))
-        produce(c, u[c][3], 0)
-        own.append(send(w.at[c, u[c][3], 0], r2.at[c, 1, 0], downs[c]))
-    for c in range(2):
-        produce(c, u[c][1], 0)
-        produce(c, u[c][3], 1)
-    for c in range(2):
-        produce(c, u[c][0], 0)
-        produce(c, u[c][0], 1)
+        for k in range(4):
+            a_up[c, order[k]], a_dn[c, order[k]] = far_copy(c, 0, k), far_copy(c, 1, k)
+    own = [near_copy(c, h) for c in range(2) for h in range(2)]
+    sent.extend(own + list(a_up.values()) + list(a_dn.values()))
     copies = [send(cnt, cntx.at[d - 1], at_x(d)) for d in (1, 2, 3)]
 
     for d in order:
@@ -309,24 +351,18 @@
         h_up[c, d] = send(piece, piece, ups[c])
         h_dn[c, d] = send(piece, piece, downs[c])
 
-    def save(piece_of):
-        pltpu.make_async_copy(piece_of(got), piece_of(out), lsem.at[8]).start()
-
     for c in range(2):
         spread(c, 0)
-        save(lambda ref: ref.at[c, us[c], :, vs[c]])
     for c in range(2):
         me = us[c]
         g_up[c].wait_recv()
         piece = got.at[c, me, 0, v[c][3]]
         f_up[c] = send(piece, piece, ups2[c])
         spread(c, 3)
-        save(lambda ref: ref.at[c, me, :, v[c][3]])
         g_dn[c].wait_recv()
         piece = got.at[c, me, 1, v[c][1]]
         f_dn[c] = send(piece, piece, downs2[c])
         spread(c, 1)
-        save(lambda ref: ref.at[c, me, :, v[c][1]])
     k_up, k_dn = {}, {}
 
     def onward(c, d):
@@ -334,11 +370,9 @@
         h_up[c, d].wait_recv()
         piece = got.at[c, u[c][3], 0, b]
         k_up[c, d] = send(piece, piece, ups[c])
-        save(lambda ref: ref.at[c, u[c][3], :, b])
         h_dn[c, d].wait_recv()
         piece = got.at[c, u[c][1], 1, b]
         k_dn[c, d] = send(piece, piece, downs[c])
-        save(lambda ref: ref.at[c, u[c][1], :, b])
 
     for c in range(2):
         onward(c, 0)
@@ -346,7 +380,6 @@
         f_up[c].wait_recv()
         f_dn[c].wait_recv()
         spread(c, 2)
-        save(lambda ref: ref.at[c, us[c], :, v[c][2]])
     for d in (3, 1, 2):
         for c in range(2):
             onward(c, d)
@@ -354,10 +387,20 @@
         for c in range(2):
             k_up[c, d].wait_recv()
             k_dn[c, d].wait_recv()
-            save(lambda ref: ref.at[c, u[c][2], :, v[c][d]])
     for copy in sent:
         copy.wait_send()
-    pltpu.make_async_copy(got, out, lsem.at[8]).wait()
+
+
+def store(got, out, sem):
+    copies = [
+        pltpu.make_async_copy(got.at[c, pl.ds(2 * h, 2)], out.at[c, pl.ds(2 * h, 2)], sem.at[2 * c + h])
+        for c in range(2)
+        for h in range(2)
+    ]
+    for copy in copies:
+        copy.start()
+    for copy in copies:
+        copy.wait()
 
 
 def body(points, centroids):
@@ -367,15 +410,14 @@
     chunk, tile = n_rows // 4, 512
     rows = n_rows // 64
     pieces = (2, 4, 2, 4, rows, width)
-    n_copies = 2 * 44 + (n_cent - 1) + 6
+    n_copies = 2 * 46 + (n_cent - 1) + 6
     vm = pltpu.VMEM
     flat = (n_rows // chunk, 1, n_points)
     scratch = [
         vm((n_points, width), BF16),
-        vm((2, n_points // 4, width), F32),
         vm((2, chunk, width), F32),
-        vm((chunk, width), BF16),
-        vm((chunk, 128), F32),
+        vm((2, chunk, width), BF16),
+        vm((2, chunk, 128), F32),
         vm((chunk, tile), F32),
         vm((chunk, tile), F32),
         vm((n_rows, n_points), BF16),
@@ -385,7 +427,6 @@
         vm((2, n_points // 128, 128), F32),
         vm((n_cent - 1, 2, n_points // 128, 128), F32),
         vm((2, 1, n_points), F32),
-        vm(pieces, F32),
         vm(pieces, F32),
         vm((2, 2, 4, rows, width), F32),
         vm((2, 2, 2, 4, rows, width), F32),
@@ -397,19 +438,27 @@
         vm((3, 16, 4, 1, 128), F32),
         pltpu.SemaphoreType.DMA((n_copies,)),
         pltpu.SemaphoreType.DMA((n_copies,)),
-        pltpu.SemaphoreType.DMA((9,)),
+        pltpu.SemaphoreType.DMA((10,)),
     ]
     result = pl.pallas_call(
         functools.partial(kernel, n_cent),
-        out_shape=jax.ShapeDtypeStruct(pieces, F32),
+        out_shape=pltpu.VMEM(pieces, F32),
         in_specs=[pl.BlockSpec(memory_space=pl.ANY)] * 2,
-        out_specs=pl.BlockSpec(memory_space=pl.ANY),
+        out_specs=pl.BlockSpec(memory_space=pltpu.VMEM),
         scratch_shapes=scratch,
         compiler_params=pltpu.CompilerParams(
-            collective_id=0, has_side_effects=True, vmem_limit_bytes=67_000_000
+            collective_id=0, has_side_effects=True, vmem_limit_bytes=50 * 2**20
         ),
-    )(points, centroids)
-    return result.reshape(n_rows, width)
+    )(points.reshape(4, 2, 4, n_points // 32, width), centroids)
+    saved = pl.pallas_call(
+        store,
+        out_shape=jax.ShapeDtypeStruct(pieces, F32),
+        in_specs=[pl.BlockSpec(memory_space=pltpu.VMEM)],
+        out_specs=pl.BlockSpec(memory_space=pl.ANY),
+        scratch_shapes=[pltpu.SemaphoreType.DMA((4,))],
+        compiler_params=pltpu.CompilerParams(vmem_limit_bytes=2**20),
+    )(result)
+    return saved.reshape(n_rows, width)
 
 
 def solution(mesh):

time: 133 us -> 122 us (0.917)
  local copies, waits for them, and re-layouts: 7.76 us -> 0 us
  Pallas kernels: 125 us -> 122 us
    unnamed x1 -> x0, local copies, waits for them, and re-layouts: 7.76 us -> none
    pallas_call x1 -> x2, Pallas kernels: 125 us -> 122 us  [the longest x1 119 us: body(): pl.pallas_call(functools.partial(kernel, n_cent), out_shape=pltpu.VMEM(pi...]
where the time goes in v2:
time: 122 us
  Pallas kernels  122 us (100%)
    pallas_call x1, Pallas kernels, body(): pl.pallas_call(functools.partial(kernel, n_cent), out_shape=pltpu.VMEM(pi...  119 us
    pallas_call x1, Pallas kernels, body(): pl.pallas_call(store, out_shape=jax.ShapeDtypeStruct(pieces, F32), in_spe...  3.37 us

profile of v2, /device:TPU:0, one launch (start us, length us, event | category | flops | bytes accessed | tf_op | source)
XLA Modules:
  0.0 121.9 jit_solution(2362585554382457034)
XLA Ops:
  0.0 118.5 %shard_map.28.got = f32[2,4,2,4,64,512]{5,4,3,2,1,0:T(8,128)S(1)} custom-call(f32[4,2,4,64,512]{4,3,2,1,0:T(8,128)} %bitcast.2, f32[4096,512]{1,0:T(8,128)} %cents.1), custom_call_target="tpu_custom_call" | custom-call | tf_op jit(solution)/shard_map/pallas_call | solution.py:443
  118.6 3.4 %shard_map.29 = f32[2,4,2,4,64,512]{5,4,3,2,1,0:T(8,128)} custom-call(f32[2,4,2,4,64,512]{5,4,3,2,1,0:T(8,128)S(1)} %shard_map.28.got), custom_call_target="tpu_custom_call" | custom-call | tf_op jit(solution)/shard_map/pallas_call | solution.py:453

commit v3 on v2

v3 whole, which is shorter than its diff:
```python
import functools

import jax
import jax.numpy as jnp
from jax import lax
from jax.experimental import pallas as pl
from jax.experimental.pallas import tpu as pltpu
from jax.sharding import PartitionSpec as P

MESH = pl.DeviceIdType.MESH
F32, BF16 = jnp.float32, jnp.bfloat16
LOG2E = 1.4426950408889634


def kernel(
    n_cent,
    points,
    cents,
    got,
    ph,
    cstage,
    ch,
    sqb,
    logit0,
    logit1,
    expo,
    mtop,
    msum,
    factor,
    stat,
    statr,
    row,
    w,
    r1,
    r2,
    t1,
    t2,
    cfin,
    cnt,
    cntx0,
    cntx1,
    cntz,
    ssem,
    rsem,
    lsem,
):
    n_points, width = ph.shape
    chunk = ch.shape[1]
    n_chunk = mtop.shape[0]
    tile = logit0.shape[1]
    n_tile = n_points // tile
    rows = w.shape[4]
    scale = LOG2E / width**0.5

    dp = lax.axis_index("dp")
    ce = lax.axis_index("cent")
    x, z = lax.rem(dp, 4), lax.div(dp, 4)

    def at_x(d):
        return (z * 4 + lax.rem(x + d, 4), ce)

    def at_z(d):
        return (lax.rem(z + d, 4) * 4 + x, ce)

    def at_cent(d):
        return (dp, lax.rem(ce + d, n_cent))

    peers = [at_x(d) for d in (1, 2, 3)] + [at_z(d) for d in (1, 2, 3)]
    peers += [at_cent(d) for d in range(1, n_cent)]
    barrier = pltpu.get_barrier_semaphore()
    for peer in peers:
        pl.semaphore_signal(barrier, inc=1, device_id=peer, device_id_type=MESH)

    used = [0]
    sent = []

    def slots(n):
        used[0] += n
        return used[0] - n

    def remote(i, src, dst, dev):
        return pltpu.make_async_remote_copy(
            src_ref=src,
            dst_ref=dst,
            send_sem=ssem.at[i],
            recv_sem=rsem.at[i],
            device_id=dev,
            device_id_type=MESH,
        )

    def send(src, dst, dev):
        copy = remote(slots(1), src, dst, dev)
        copy.start()
        sent.append(copy)
        return copy

    part = n_points // 4

    def load_points(i):
        return pltpu.make_async_copy(
            points.at[i], w.at[0, i], lsem.at[i]
        )

    def load_cents(i):
        slot = lax.rem(i, 2)
        return pltpu.make_async_copy(
            cents.at[pl.ds(i * chunk, chunk)], cstage.at[slot], lsem.at[4 + slot]
        )

    load_points(0).start()
    load_cents(0).start()
    load_cents(1).start()
    for i in range(1, 4):
        load_points(i).start()

    def round_points(i):
        load_points(i).wait()
        ph[i * part : (i + 1) * part, :] = w[0, i].reshape(part, width).astype(BF16)

    def round_cents(i):
        load_cents(i).wait()
        value = cstage[i % 2]
        ch[i] = value.astype(BF16)
        sqb[i] = jnp.broadcast_to(
            jnp.sum(value * value, axis=1, keepdims=True) * scale, (chunk, 128)
        )
        if i + 2 < n_chunk:
            load_cents(i + 2).start()

    def span(t):
        return pl.ds(pl.multiple_of(t * tile, tile), tile)

    def first(t, c, logit):
        inner = lax.dot_general(
            ch[c], ph[span(t), :], (((1,), (1,)), ((), ())), preferred_element_type=F32
        )
        value = inner * (2.0 * scale) - jnp.concatenate([sqb[c]] * (tile // 128), axis=1)
        logit[...] = value
        return jnp.max(value, axis=0, keepdims=True)

    def second(t, c, logit, high):
        e = jnp.exp2(logit[...] - high)
        expo[c * chunk : (c + 1) * chunk, span(t)] = e.astype(BF16)
        mtop[c, :, span(t)] = high
        msum[c, :, span(t)] = jnp.sum(e, axis=0, keepdims=True)

    stats = slots(n_tile * (n_cent - 1))

    def stat_copy(t, d):
        i = stats + t * (n_cent - 1) + d - 1
        return remote(i, stat.at[t], statr.at[d - 1, t], at_cent(d))

    def local_stats(t):
        tops = [mtop[c, :, span(t)] for c in range(n_chunk)]
        top = functools.reduce(jnp.maximum, tops)
        total = sum(msum[c, :, span(t)] * jnp.exp2(tops[c] - top) for c in range(n_chunk))
        for i in range(tile // 128):
            stat[t, 0, i : i + 1, :] = top[:, i * 128 : (i + 1) * 128]
            stat[t, 1, i : i + 1, :] = total[:, i * 128 : (i + 1) * 128]
        for d in range(1, n_cent):
            stat_copy(t, d).start()

    logits = (logit0, logit1)

    def on_tile(t, high, start=False, last=False):
        for c in range(n_chunk):
            after = None
            if c + 1 < n_chunk:
                after = first(t, c + 1, logits[(c + 1) % 2])
            elif not last:
                after = first(t + 1, 0, logits[(c + 1) % 2])
            if start and c + 2 < n_chunk:
                round_cents(c + 2)
            if start and c + 1 < n_tile:
                round_points(c + 1)
            second(t, c, logits[c % 2], high)
            high = after
        if start:
            pl.semaphore_wait(barrier, len(peers))
        local_stats(t)
        return high

    round_points(0)
    round_cents(0)
    high = first(0, 0, logit0)
    round_cents(1)
    high = on_tile(0, high, start=True)
    high = lax.fori_loop(1, n_tile - 1, on_tile, high)
    on_tile(n_tile - 1, high, last=True)
    sent.extend(stat_copy(t, d) for t in range(n_tile) for d in range(1, n_cent))

    def absorb(t):
        for d in range(1, n_cent):
            stat_copy(t, d).wait_recv()
        tops = [stat[t, 0]] + [statr[d, t, 0] for d in range(n_cent - 1)]
        sums = [stat[t, 1]] + [statr[d, t, 1] for d in range(n_cent - 1)]
        high = functools.reduce(jnp.maximum, tops)
        inverse = 1.0 / sum(s * jnp.exp2(t - high) for t, s in zip(tops, sums))
        for i in range(tile // 128):
            at = slice(t * tile + i * 128, t * tile + (i + 1) * 128)
            row[0, :, at] = high[i : i + 1, :]
            row[1, :, at] = inverse[i : i + 1, :]
        at = slice(t * tile, (t + 1) * tile)
        for c in range(n_chunk):
            factor[c, :, at] = jnp.exp2(mtop[c, :, at] - row[0, :, at]) * row[1, :, at]

    us, vs = (x, z), (z, x)
    fins = []
    for c in range(2):
        for h in range(2):
            at = ((c * 4 + us[c]) * 2 + h) * (4 * rows) + vs[c] * rows
            fins.append(
                pltpu.make_async_copy(
                    cents.at[pl.ds(pl.multiple_of(at, rows), rows)],
                    cfin.at[c, h],
                    lsem.at[6 + 2 * c + h],
                )
            )
            fins[-1].start()

    def produce(c, bu, h, tiles, fresh):
        block = (c * 4 + bu) * 2 + h
        at = pl.multiple_of(block * (4 * rows), 4 * rows)
        group = lax.div(block * (4 * rows), chunk)
        acc = jnp.zeros((4 * rows, width), F32)
        count = jnp.zeros((4 * rows, 128), F32)
        for t in tiles:
            cols = slice(t * tile, (t + 1) * tile)
            resp = (expo[pl.ds(at, 4 * rows), cols].astype(F32) * factor[group, :, cols]).astype(BF16)
            acc += jnp.dot(resp, ph[cols, :], preferred_element_type=F32)
            wide = resp.astype(F32)
            for l in range(tile // 128):
                count += wide[:, l * 128 : (l + 1) * 128]
        acc = acc.reshape(4, rows, width)
        w[c, bu, h] = acc if fresh else w[c, bu, h] + acc
        line = jnp.sum(count.T, axis=0, keepdims=True)
        for b in range(4):
            part = line[:, b * rows : (b + 1) * rows]
            cnt[block, b, :, :rows] = part if fresh else cnt[block, b, :, :rows] + part

    ups = (at_x(1), at_z(1))
    downs = (at_x(3), at_z(3))
    u = [[lax.rem(us[c] + d, 4) for d in range(4)] for c in range(2)]
    v = [[lax.rem(vs[c] + d, 4) for d in range(4)] for c in range(2)]
    order = (2, 1, 3, 0)

    def place(c):
        return x * (1 - c) + z * c, z * (1 - c) + x * c

    def along(c, d):
        return (lax.rem(z + c * d, 4) * 4 + lax.rem(x + (1 - c) * d, 4), ce)

    far, near = slots(16), slots(4)

    def far_copy(c, h, k):
        here, other = place(c)
        b = lax.rem(other + order[k], 4)
        return remote(
            far + (c * 2 + h) * 4 + k,
            w.at[c, lax.rem(here + 2, 4), h, b],
            r1.at[c, h, b],
            along(c, 1 + 2 * h),
        )

    def near_copy(c, h):
        here, _ = place(c)
        d = 3 - 2 * h
        return remote(
            near + c * 2 + h, w.at[c, lax.rem(here + d, 4), h], r2.at[c, 1 - h, h], along(c, d)
        )

    def begin(i, carry):
        c, h = lax.rem(i, 2), lax.div(i, 2)
        produce(c, lax.rem(place(c)[0] + 2, 4), h, range(n_tile - 1), True)
        return carry

    def farthest(i, carry):
        c, h = lax.rem(i, 2), lax.div(i, 2)
        produce(c, lax.rem(place(c)[0] + 2, 4), h, [n_tile - 1], False)
        for k in range(4):
            far_copy(c, h, k).start()
        return carry

    def nearest(i, carry):
        c, h = lax.rem(i, 2), 1 - lax.div(i, 2)
        produce(c, lax.rem(place(c)[0] + 3 - 2 * h, 4), h, range(n_tile), True)
        near_copy(c, h).start()
        return carry

    def others(i, carry):
        c, h, mine = lax.rem(i, 2), lax.rem(lax.div(i, 2), 2), lax.div(i, 4)
        produce(c, lax.rem(place(c)[0] + (1 - mine) * (1 + 2 * h), 4), h, range(n_tile), True)
        return carry

    for t in range(n_tile - 1):
        absorb(t)
    lax.fori_loop(0, 4, begin, 0)
    absorb(n_tile - 1)
    lax.fori_loop(0, 4, farthest, 0)
    lax.fori_loop(0, 4, nearest, 0)
    lax.fori_loop(0, 8, others, 0)
    a_up, a_dn, b_up, b_dn = {}, {}, {}, {}
    for c in range(2):
        for k in range(4):
            a_up[c, order[k]], a_dn[c, order[k]] = far_copy(c, 0, k), far_copy(c, 1, k)
    own = [near_copy(c, h) for c in range(2) for h in range(2)]
    sent.extend(own + list(a_up.values()) + list(a_dn.values()))
    copies = []
    for d in (1, 2, 3):
        to = lax.rem(x + d, 4)
        copies.append(send(cnt.at[pl.ds(2 * to, 2)], cntx0.at[d - 1], at_x(d)))
        copies.append(send(cnt.at[pl.ds(8, 8), to], cntx1.at[d - 1], at_x(d)))

    for d in order:
        for c in range(2):
            b = v[c][d]
            a_up[c, d].wait_recv()
            w[c, u[c][1], 0, b] += r1[c, 0, b]
            b_up[c, d] = send(w.at[c, u[c][1], 0, b], r2.at[c, 0, 0, b], ups[c])
            a_dn[c, d].wait_recv()
            w[c, u[c][3], 1, b] += r1[c, 1, b]
            b_dn[c, d] = send(w.at[c, u[c][3], 1, b], r2.at[c, 1, 1, b], downs[c])
    for copy in copies:
        copy.wait_recv()
    mine = pl.ds(2 * x, 2)
    cnt[mine] = cnt[mine] + cntx0[0] + cntx0[1] + cntx0[2]
    cnt[8:16, x] = cnt[8:16, x] + cntx1[0] + cntx1[1] + cntx1[2]
    copies = []
    for d in (1, 2, 3):
        to = lax.rem(z + d, 4)
        copies.append(send(cnt.at[mine, to], cntz.at[0, d - 1], at_z(d)))
        copies.append(send(cnt.at[pl.ds(8 + 2 * to, 2), x], cntz.at[1, d - 1], at_z(d)))
    for copy in own:
        copy.wait_recv()

    ups2, downs2 = ups[::-1], downs[::-1]
    halves = [pl.ds(q * (rows // 2), rows // 2) for q in range(2)]
    s_up, s_dn, ends = {}, {}, ([], [])

    def pass_on(c, h, d, q):
        side = h if d is None else 1 - h
        to = (ups2, downs2)[side][c]
        b = v[c][d or (1 + 2 * h)]
        ends[q].append(
            send(w.at[c, us[c], h, b, halves[q]], t2.at[c, side, h, halves[q]], to)
        )

    for d in order:
        for c in range(2):
            b, me = v[c][d], us[c]
            b_up[c, d].wait_recv()
            b_dn[c, d].wait_recv()
            for h in range(2):
                w[c, me, h, b] += r2[c, 0, h, b] + r2[c, 1, h, b]
            if d == 2:
                for q in range(2):
                    part = halves[q]
                    s_up[c, q] = send(w.at[c, me, 0, b, part], t1.at[c, 0, part], ups2[c])
                    s_dn[c, q] = send(w.at[c, me, 1, b, part], t1.at[c, 1, part], downs2[c])
            if d == 1:
                pass_on(c, 1, 1, 0)
            if d == 3:
                pass_on(c, 0, 3, 0)
    for q in range(2):
        if q == 1:
            for c in range(2):
                pass_on(c, 1, 1, 1)
                pass_on(c, 0, 3, 1)
        for c in range(2):
            me, part = us[c], halves[q]
            s_up[c, q].wait_recv()
            w[c, me, 0, v[c][1], part] += t1[c, 0, part]
            pass_on(c, 0, None, q)
            s_dn[c, q].wait_recv()
            w[c, me, 1, v[c][3], part] += t1[c, 1, part]
            pass_on(c, 1, None, q)

    for copy in copies:
        copy.wait_recv()
    for copy in fins:
        copy.wait()
    counts = {}
    for c in range(2):
        for h in range(2):
            line = cnt[(c * 4 + us[c]) * 2 + h, vs[c]]
            line = line + cntz[c, 0, h] + cntz[c, 1, h] + cntz[c, 2, h]
            counts[c, h] = jnp.broadcast_to(line, (128, 128)).T + 1.0
    g_up, g_dn, h_up, h_dn, f_up, f_dn = {}, {}, {}, {}, {}, {}
    for q in range(2):
        for copy in ends[q]:
            copy.wait_recv()
        part = halves[q]
        for c in range(2):
            me, b = us[c], vs[c]
            for h in range(2):
                count = counts[c, h][q * (rows // 2) : (q + 1) * (rows // 2)]
                count = jnp.concatenate([count] * (width // 128), axis=1)
                value = w[c, me, h, b, part] + t2[c, 0, h, part] + t2[c, 1, h, part]
                got[c, me, h, b, part] = (value + cfin[c, h, part]) / count
            mine = got.at[c, me, :, b, part]
            g_up[c, q] = send(mine, mine, ups2[c])
            g_dn[c, q] = send(mine, mine, downs2[c])
        for c in range(2):
            mine = got.at[c, us[c], :, vs[c], part]
            h_up[c, q] = send(mine, mine, ups[c])
            h_dn[c, q] = send(mine, mine, downs[c])

    e_up, e_dn = {}, {}

    def spread(c, d):
        piece = got.at[c, us[c], :, v[c][d]]
        e_up[c, d] = send(piece, piece, ups[c])
        e_dn[c, d] = send(piece, piece, downs[c])

    for c in range(2):
        me = us[c]
        g_up[c, 0].wait_recv()
        g_up[c, 1].wait_recv()
        piece = got.at[c, me, 0, v[c][3]]
        f_up[c] = send(piece, piece, ups2[c])
        spread(c, 3)
        g_dn[c, 0].wait_recv()
        g_dn[c, 1].wait_recv()
        piece = got.at[c, me, 1, v[c][1]]
        f_dn[c] = send(piece, piece, downs2[c])
        spread(c, 1)
    k_up, k_dn = {}, {}

    def onward(c, d):
        b = v[c][d]
        for copy in [h_up[c, 0], h_up[c, 1]] if d == 0 else [e_up[c, d]]:
            copy.wait_recv()
        piece = got.at[c, u[c][3], 0, b]
        k_up[c, d] = send(piece, piece, ups[c])
        for copy in [h_dn[c, 0], h_dn[c, 1]] if d == 0 else [e_dn[c, d]]:
            copy.wait_recv()
        piece = got.at[c, u[c][1], 1, b]
        k_dn[c, d] = send(piece, piece, downs[c])

    for c in range(2):
        onward(c, 0)
    for c in range(2):
        f_up[c].wait_recv()
        f_dn[c].wait_recv()
        spread(c, 2)
    for d in (3, 1, 2):
        for c in range(2):
            onward(c, d)
    for d in (0, 3, 1, 2):
        for c in range(2):
            k_up[c, d].wait_recv()
            k_dn[c, d].wait_recv()
    for copy in sent:
        copy.wait_send()


def store(got, out, sem):
    copies = [
        pltpu.make_async_copy(got.at[c, pl.ds(2 * h, 2)], out.at[c, pl.ds(2 * h, 2)], sem.at[2 * c + h])
        for c in range(2)
        for h in range(2)
    ]
    for copy in copies:
        copy.start()
    for copy in copies:
        copy.wait()


def body(points, centroids):
    n_points, width = points.shape
    n_rows = centroids.shape[0]
    n_cent = lax.axis_size("cent")
    chunk, tile = n_rows // 4, 512
    rows = n_rows // 64
    pieces = (2, 4, 2, 4, rows, width)
    n_copies = 2 * 54 + 4 * (n_cent - 1) + 12
    vm = pltpu.VMEM
    flat = (n_rows // chunk, 1, n_points)
    scratch = [
        vm((n_points, width), BF16),
        vm((2, chunk, width), F32),
        vm((n_rows // chunk, chunk, width), BF16),
        vm((n_rows // chunk, chunk, 128), F32),
        vm((chunk, tile), F32),
        vm((chunk, tile), F32),
        vm((n_rows, n_points), BF16),
        vm(flat, F32),
        vm(flat, F32),
        vm(flat, F32),
        vm((n_points // tile, 2, tile // 128, 128), F32),
        vm((n_cent - 1, n_points // tile, 2, tile // 128, 128), F32),
        vm((2, 1, n_points), F32),
        vm(pieces, F32),
        vm((2, 2, 4, rows, width), F32),
        vm((2, 2, 2, 4, rows, width), F32),
        vm((2, 2, rows, width), F32),
        vm((2, 2, 2, rows, width), F32),
        vm((2, 2, rows, width), F32),
        vm((16, 4, 1, 128), F32),
        vm((3, 2, 4, 1, 128), F32),
        vm((3, 8, 1, 128), F32),
        vm((2, 3, 2, 1, 128), F32),
        pltpu.SemaphoreType.DMA((n_copies,)),
        pltpu.SemaphoreType.DMA((n_copies,)),
        pltpu.SemaphoreType.DMA((10,)),
    ]
    result = pl.pallas_call(
        functools.partial(kernel, n_cent),
        out_shape=pltpu.VMEM(pieces, F32),
        in_specs=[pl.BlockSpec(memory_space=pl.ANY)] * 2,
        out_specs=pl.BlockSpec(memory_space=pltpu.VMEM),
        scratch_shapes=scratch,
        compiler_params=pltpu.CompilerParams(
            collective_id=0, has_side_effects=True, vmem_limit_bytes=54 * 2**20
        ),
    )(points.reshape(4, 2, 4, n_points // 32, width), centroids)
    saved = pl.pallas_call(
        store,
        out_shape=jax.ShapeDtypeStruct(pieces, F32),
        in_specs=[pl.BlockSpec(memory_space=pltpu.VMEM)],
        out_specs=pl.BlockSpec(memory_space=pl.ANY),
        scratch_shapes=[pltpu.SemaphoreType.DMA((4,))],
        compiler_params=pltpu.CompilerParams(vmem_limit_bytes=2**20),
    )(result)
    return saved.reshape(n_rows, width)


def solution(mesh):
    placed = (P("dp", None), P("cent", None))
    return jax.shard_map(
        body, mesh=mesh, in_specs=placed, out_specs=P("cent", None), check_vma=False
    )
```

time: 122 us -> 119 us (0.975)
  Pallas kernels: 122 us -> 119 us
    pallas_call x1, Pallas kernels: 119 us -> 115 us  [body(): pl.pallas_call(functools.partial(kernel, n_cent), out_shape=pltpu.VMEM(pi...]
where the time goes in v3:
time: 119 us
  Pallas kernels  119 us (100%)
    pallas_call x1, Pallas kernels, body(): pl.pallas_call(functools.partial(kernel, n_cent), out_shape=pltpu.VMEM(pi...  115 us
    pallas_call x1, Pallas kernels, body(): pl.pallas_call(store, out_shape=jax.ShapeDtypeStruct(pieces, F32), in_spe...  3.37 us

profile of v3, /device:TPU:0, one launch (start us, length us, event | category | flops | bytes accessed | tf_op | source)
XLA Modules:
  0.0 119.0 jit_solution(8522041448483949319)
XLA Ops:
  0.0 115.5 %shard_map.28.got = f32[2,4,2,4,64,512]{5,4,3,2,1,0:T(8,128)S(1)} custom-call(f32[4,2,4,64,512]{4,3,2,1,0:T(8,128)} %bitcast.2, f32[4096,512]{1,0:T(8,128)} %cents.1), custom_call_target="tpu_custom_call" | custom-call | tf_op jit(solution)/shard_map/pallas_call | solution.py:507
  115.5 3.4 %shard_map.29 = f32[2,4,2,4,64,512]{5,4,3,2,1,0:T(8,128)} custom-call(f32[2,4,2,4,64,512]{5,4,3,2,1,0:T(8,128)S(1)} %shard_map.28.got), custom_call_target="tpu_custom_call" | custom-call | tf_op jit(solution)/shard_map/pallas_call | solution.py:517

commit v4 on v2

v4 whole, which is shorter than its diff:
```python
import functools

import jax
import jax.numpy as jnp
from jax import lax
from jax.experimental import pallas as pl
from jax.experimental.pallas import tpu as pltpu
from jax.sharding import PartitionSpec as P

MESH = pl.DeviceIdType.MESH
F32, BF16 = jnp.float32, jnp.bfloat16
LOG2E = 1.4426950408889634


def kernel(
    n_cent,
    points,
    cents,
    got,
    ph,
    pho,
    pin,
    cstage,
    ch,
    sqb,
    logit0,
    logit1,
    expo,
    mtop,
    msum,
    factor,
    stat,
    statr,
    row,
    rowo,
    w,
    x1,
    x2,
    r1,
    r2,
    t1,
    t2,
    cfin,
    cnt,
    cx0,
    cx1,
    cntz,
    ssem,
    rsem,
    lsem,
):
    n_points, width = ph.shape
    chunk = cstage.shape[1]
    n_chunk = mtop.shape[0]
    tile = logit0.shape[1]
    n_tile = n_points // tile
    rows = w.shape[2]
    scale = LOG2E / width**0.5

    dp = lax.axis_index("dp")
    ce = lax.axis_index("cent")
    x, z = lax.rem(dp, 4), lax.div(dp, 4)

    y, core = lax.div(ce, 2), lax.rem(ce, 2)

    def slot_of(x):
        return 2 * lax.rem(lax.div(x + 1, 2), 2) + lax.div(x, 2)

    half, g = lax.rem(lax.div(x + 1, 2), 2), lax.div(x, 2)
    slot = slot_of(x)
    friend = (z * 4 + x + 1 - 2 * lax.rem(x, 2), ce)
    mate = (z * 4 + 3 - x, ce)

    def at_y(d):
        return (dp, lax.rem(y + d, 4) * 2 + core)

    sibling = (dp, y * 2 + 1 - core)

    def at_x(d):
        return (z * 4 + lax.rem(x + d, 4), ce)

    def at_z(d):
        return (lax.rem(z + d, 4) * 4 + x, ce)

    def at_cent(d):
        return (dp, lax.rem(ce + d, n_cent))

    peers = [at_x(d) for d in (1, 3)] + [at_z(d) for d in (1, 2, 3)]
    peers += [at_cent(d) for d in range(1, n_cent)]
    barrier = pltpu.get_barrier_semaphore()
    for peer in peers:
        pl.semaphore_signal(barrier, inc=1, device_id=peer, device_id_type=MESH)

    used = [0]
    sent = []

    def slots(n):
        used[0] += n
        return used[0] - n

    def remote(i, src, dst, dev):
        return pltpu.make_async_remote_copy(
            src_ref=src,
            dst_ref=dst,
            send_sem=ssem.at[i],
            recv_sem=rsem.at[i],
            device_id=dev,
            device_id_type=MESH,
        )

    def send(src, dst, dev):
        copy = remote(slots(1), src, dst, dev)
        copy.start()
        sent.append(copy)
        return copy

    part = n_points // 4

    def load_points(i):
        return pltpu.make_async_copy(
            points.at[pl.ds(2 * i, 2)], w.at[pl.ds(2 * i, 2)], lsem.at[i]
        )

    def load_cents(i):
        return pltpu.make_async_copy(
            cents.at[pl.ds(i * chunk, chunk)], cstage.at[i % 2], lsem.at[4 + i % 2]
        )

    for i in range(4):
        load_points(i).start()
    load_cents(0).start()
    load_cents(1).start()

    def round_cents(i):
        value = cstage[i % 2]
        ch[i * chunk : (i + 1) * chunk, :] = value.astype(BF16)
        sqb[i * chunk : (i + 1) * chunk, :] = jnp.broadcast_to(
            jnp.sum(value * value, axis=1, keepdims=True) * scale, (chunk, 128)
        )

    def first(c, t, logit):
        at = slice(c * chunk, (c + 1) * chunk)
        inner = lax.dot_general(
            ch[at, :], ph[t * tile : (t + 1) * tile, :], (((1,), (1,)), ((), ())),
            preferred_element_type=F32,
        )
        value = inner * (2.0 * scale) - jnp.concatenate([sqb[at, :]] * (tile // 128), axis=1)
        logit[...] = value
        return jnp.max(value, axis=0, keepdims=True)

    def second(c, t, logit, high):
        at = slice(t * tile, (t + 1) * tile)
        e = jnp.exp2(logit[...] - high)
        expo[c * chunk : (c + 1) * chunk, at] = e.astype(BF16)
        mtop[c, :, at] = high
        msum[c, :, at] = jnp.sum(e, axis=0, keepdims=True)

    across = lax.rem(y + 2, 4) * 2 + core
    behind, ahead = lax.rem(y + 3, 4) * 2 + core, lax.rem(y + 1, 4) * 2 + core
    bring, go_up, go_dn, turn, side = slots(6), slots(4), slots(4), slots(2), slots(16)

    def bring_copy(i):
        if i < 4:
            return remote(bring + i, w.at[ce, i], pin.at[ce, i], friend)
        return remote(bring + i, points.at[across, i - 2], pin.at[across, i - 2], friend)

    def up_copy(i):
        return remote(go_up + i, pin.at[ce, i], pin.at[ce, i], at_y(1))

    def dn_copy(i):
        return remote(go_dn + i, pin.at[ce, i], pin.at[ce, i], at_y(3))

    def turn_copy(i):
        at, to = ((behind, at_y(1)), (ahead, at_y(3)))[i]
        return remote(turn + i, pin.at[at, i], pin.at[at, i], to)

    def side_copy(k, i):
        at = (ce, ahead, across, behind)[k]
        return remote(side + 4 * k + i, pin.at[at, i], pin.at[at, i], sibling)

    def start(copy):
        copy.start()
        sent.append(copy)

    def import_all():
        pl.semaphore_wait(barrier, len(peers))
        for i in range(6):
            bring_copy(i).start()
        sent.extend(bring_copy(i) for i in (4, 5))

    def relay(i):
        bring_copy(i).wait_recv()
        start(up_copy(i))
        start(dn_copy(i))
        start(side_copy(0, i))

    def relay_next(i):
        up_copy(i).wait_recv()
        if i == 0:
            start(turn_copy(0))
        start(side_copy(3, i))
        dn_copy(i).wait_recv()
        if i == 1:
            start(turn_copy(1))
        start(side_copy(1, i))

    def relay_far(i):
        (turn_copy(i) if i < 2 else bring_copy(i + 2)).wait_recv()
        start(side_copy(2, i))

    events = {1: import_all, 9: lambda: relay(0), 13: lambda: relay(1)}
    logits = (logit0, logit1)
    for i in range(4):
        load_points(i).wait()
        ph[i * part : (i + 1) * part, :] = w[2 * i : 2 * i + 2].reshape(part, width).astype(BF16)
        if i == 0:
            load_cents(0).wait()
            round_cents(0)
    high = first(0, 0, logit0)
    for c in range(n_chunk):
        last = c + 1 == n_chunk
        if not last:
            load_cents(c + 1).wait()
            if c + 2 < n_chunk:
                load_cents(c + 2).start()
        for t in range(n_tile):
            after = None
            if t + 1 < n_tile:
                after = first(c, t + 1, logits[(t + 1) % 2])
                if t == 0 and not last:
                    round_cents(c + 1)
            elif not last:
                after = first(c + 1, 0, logits[(t + 1) % 2])
            second(c, t, logits[t % 2], high)
            high = after
            events.get(c * n_tile + t, lambda: None)()

    stats = slots(n_cent - 1)

    def stat_copy(d):
        return remote(stats + d - 1, stat, statr.at[d - 1], at_cent(d))

    top = functools.reduce(jnp.maximum, [mtop[c] for c in range(n_chunk)])
    total = sum(msum[c] * jnp.exp2(mtop[c] - top) for c in range(n_chunk))
    for i in range(n_points // 128):
        stat[0, i : i + 1, :] = top[:, i * 128 : (i + 1) * 128]
        stat[1, i : i + 1, :] = total[:, i * 128 : (i + 1) * 128]
    for d in range(1, n_cent):
        stat_copy(d).start()
    sent.extend(stat_copy(d) for d in range(1, n_cent))

    def absorb():
        for d in range(1, n_cent):
            stat_copy(d).wait_recv()
        tops = [stat[0]] + [statr[d, 0] for d in range(n_cent - 1)]
        sums = [stat[1]] + [statr[d, 1] for d in range(n_cent - 1)]
        high = functools.reduce(jnp.maximum, tops)
        inverse = 1.0 / sum(s * jnp.exp2(t - high) for t, s in zip(tops, sums))
        for i in range(n_points // 128):
            row[0, :, i * 128 : (i + 1) * 128] = high[i : i + 1, :]
            row[1, :, i * 128 : (i + 1) * 128] = inverse[i : i + 1, :]
        for c in range(n_chunk):
            factor[c] = jnp.exp2(mtop[c] - row[0]) * row[1]

    us, vs = (slot, z), (z, slot)
    fins = []
    for c in range(2):
        for h in range(2):
            at = ((c * 4 + us[c]) * 2 + h) * (4 * rows) + vs[c] * rows
            fins.append(
                pltpu.make_async_copy(
                    cents.at[pl.ds(pl.multiple_of(at, rows), rows)],
                    cfin.at[c, h],
                    lsem.at[6 + 2 * c + h],
                )
            )
            fins[-1].start()

    def own_row(i):
        c = lax.div(i, 4)
        return (
            c,
            (1 - c) * ((4 * half + i) * 4 * rows)
            + c * (32 * rows + (i - 4) * 8 * rows + half * 2 * rows),
        )

    def gather(ref, i, cols):
        c, at = own_row(i)
        at = pl.multiple_of(at, 2 * rows)
        low = ref[pl.ds(at, 2 * rows), cols]
        at = pl.multiple_of(at + (1 + c) * 2 * rows, 2 * rows)
        return jnp.concatenate([low, ref[pl.ds(at, 2 * rows), cols]], axis=0)

    def add_up(count, resp):
        wide = resp.astype(F32)
        for l in range(tile // 128):
            count += wide[:, l * 128 : (l + 1) * 128]
        return count

    def put(i, acc, count, fresh):
        acc = acc.reshape(4, rows, width)
        w[i] = acc if fresh else w[i] + acc
        line = jnp.sum(count.T, axis=0, keepdims=True)
        for b in range(4):
            piece = line[:, b * rows : (b + 1) * rows]
            cnt[i, b, :, :rows] = piece if fresh else cnt[i, b, :, :rows] + piece

    def with_own(i, carry):
        group = lax.div(own_row(i)[1], chunk)
        acc = jnp.zeros((4 * rows, width), F32)
        count = jnp.zeros((4 * rows, 128), F32)
        for t in range(n_tile):
            cols = slice(t * tile, (t + 1) * tile)
            resp = (gather(expo, i, cols).astype(F32) * factor[group, :, cols]).astype(BF16)
            acc += jnp.dot(resp, ph[cols, :], preferred_element_type=F32)
            count = add_up(count, resp)
        put(i, acc, count, True)
        return carry

    everything = slice(None)

    def with_other(i, steps):
        acc = jnp.zeros((4 * rows, width), F32)
        count = jnp.zeros((4 * rows, 128), F32)
        cent = gather(ch, i, everything)
        square = jnp.concatenate([gather(sqb, i, everything)] * (tile // 128), axis=1)
        for d in steps:
            cols = pl.ds(pl.multiple_of(lax.rem(y + d, 4) * tile, tile), tile)
            inner = lax.dot_general(
                cent, pho[cols, :], (((1,), (1,)), ((), ())), preferred_element_type=F32
            )
            value = inner * (2.0 * scale) - square - rowo[0, :, cols]
            resp = (jnp.exp2(value) * rowo[1, :, cols]).astype(BF16)
            acc += jnp.dot(resp, pho[cols, :], preferred_element_type=F32)
            count = add_up(count, resp)
        put(i, acc, count, False)

    def round_other(d):
        for i in range(4):
            side_copy(d, i).wait_recv()
        at = lax.rem(y + d, 4)
        value = pin[pl.ds(2 * at, 2)].reshape(tile, width)
        pho[pl.ds(pl.multiple_of(at * tile, tile), tile), :] = value.astype(BF16)

    relay(2)
    relay_next(0)
    relay(3)
    relay_next(1)
    absorb()
    rows_copy = send(row, rowo, friend)
    for i in range(4):
        bring_copy(i).wait_send()
    lax.fori_loop(0, 2, with_own, 0)
    relay_next(2)
    relay_far(2)
    lax.fori_loop(2, 4, with_own, 0)
    relay_far(0)
    relay_far(1)
    relay_far(3)
    lax.fori_loop(4, 8, with_own, 0)
    relay_next(3)
    rows_copy.wait_recv()

    ups = (at_x(1), at_z(1))
    downs = (at_x(3), at_z(3))
    xs = [slot_of(lax.rem(x + d, 4)) for d in range(4)]
    zs = [lax.rem(z + d, 4) for d in range(4)]
    u, v = (xs, zs), (zs, xs)
    order = (2, 1, 3, 0)
    theirs, mine = 1 - g, g

    def to_mate(h):
        for d in order:
            over[h, d] = send(w.at[theirs * 2 + h, zs[d]], x1.at[h, zs[d]], mate)

    over = {}
    early = (0, 1, 3)
    for d in early:
        round_other(d)
    with_other(theirs * 2, early)
    with_other(4 + zs[2], early)
    round_other(2)
    with_other(theirs * 2, (2,))
    to_mate(0)
    with_other(4 + zs[2], (2,))
    a_up = send(w.at[4 + zs[2], pl.ds(0, 2)], r1.at[0], ups[1])
    a_dn = send(w.at[4 + zs[2], pl.ds(2, 2)], r1.at[1], downs[1])
    with_other(theirs * 2 + 1, range(4))
    to_mate(1)
    with_other(4 + zs[1], range(4))
    n_up = send(w.at[4 + zs[1], pl.ds(2, 2)], r2.at[0, 1], ups[1])
    with_other(4 + zs[3], range(4))
    n_dn = send(w.at[4 + zs[3], pl.ds(0, 2)], r2.at[1, 0], downs[1])

    def rest(i, carry):
        top = lax.div(3 - i, 3)
        with_other(top * (4 + z) + (1 - top) * (mine * 2 + i - 1), range(4))
        return carry

    lax.fori_loop(0, 3, rest, 0)

    a_up.wait_recv()
    b_up, b_dn = [], []
    sides = (theirs, mine)
    for k in sides:
        w[4 + zs[1], k] += r1[0, k]
        b_up.append(send(w.at[4 + zs[1], k], r2.at[0, 0, k], ups[1]))
    a_dn.wait_recv()
    for k in sides:
        w[4 + zs[3], 2 + k] += r1[1, k]
        b_dn.append(send(w.at[4 + zs[3], 2 + k], r2.at[1, 1, k], downs[1]))

    copies = [send(cnt.at[pl.ds(theirs * 2, 2)], cx0, mate)]
    for h in range(2):
        copies.append(send(cnt.at[pl.ds(4, 4), 2 * h + theirs], cx1.at[h], mate))
    for copy in copies:
        copy.wait_recv()
    block = pl.ds(2 * mine, 2)
    cnt[block] = cnt[block] + cx0[...]
    for h in range(2):
        cnt[4:8, 2 * h + mine] = cnt[4:8, 2 * h + mine] + cx1[h]
    copies = []
    for d in (1, 2, 3):
        copies.append(send(cnt.at[block, zs[d]], cntz.at[0, d - 1], at_z(d)))
        for h in range(2):
            copies.append(
                send(cnt.at[4 + zs[d], 2 * h + mine], cntz.at[1, d - 1, h], at_z(d))
            )

    halves = [pl.ds(q * (rows // 2), rows // 2) for q in range(2)]
    s_up, s_dn, ends = {}, {}, ([], [])

    def pass_on(h, d, q):
        lane = h if d is None else 1 - h
        to = (ups[1], downs[1])[lane]
        b = zs[d or (1 + 2 * h)]
        ends[q].append(
            send(w.at[mine * 2 + h, b, halves[q]], t2.at[lane, h, halves[q]], to)
        )

    def settle(k, n):
        b_up[n].wait_recv()
        b_dn[n].wait_recv()
        for h in range(2):
            w[4 + z, 2 * h + k] += r2[0, h, k] + r2[1, h, k]

    last = []
    for d in order:
        for h in range(2):
            over[h, d].wait_recv()
            w[mine * 2 + h, zs[d]] += x1[h, zs[d]]
        if d == 2:
            for q in range(2):
                part = halves[q]
                s_up[q] = send(w.at[mine * 2, zs[2], part], t1.at[0, part], ups[1])
                s_dn[q] = send(w.at[mine * 2 + 1, zs[2], part], t1.at[1, part], downs[1])
            n_up.wait_recv()
            n_dn.wait_recv()
            settle(theirs, 0)
            for h in range(2):
                last.append(send(w.at[4 + z, 2 * h + theirs], x2.at[h], mate))
        if d == 1:
            pass_on(1, 1, 0)
        if d == 3:
            pass_on(0, 3, 0)
            settle(mine, 1)
    for q in range(2):
        if q == 1:
            pass_on(1, 1, 1)
            pass_on(0, 3, 1)
        part = halves[q]
        s_up[q].wait_recv()
        w[mine * 2, zs[1], part] += t1[0, part]
        pass_on(0, None, q)
        s_dn[q].wait_recv()
        w[mine * 2 + 1, zs[3], part] += t1[1, part]
        pass_on(1, None, q)

    for copy in copies:
        copy.wait_recv()
    for copy in fins:
        copy.wait()
    g_up, g_dn, h_up, h_dn, f_up, f_dn = {}, {}, {}, {}, {}, {}
    for c in range(2):
        counts = []
        for h in range(2):
            line = cnt[mine * 2 + h, z] if c == 0 else cnt[4 + z, 2 * h + mine]
            line = line + cntz[c, 0, h] + cntz[c, 1, h] + cntz[c, 2, h]
            counts.append(jnp.broadcast_to(line, (128, 128)).T + 1.0)
        for q in range(2):
            part = halves[q]
            if c == 0 or q == 0:
                for copy in last if c else ends[q]:
                    copy.wait_recv()
            for h in range(2):
                count = counts[h][q * (rows // 2) : (q + 1) * (rows // 2)]
                count = jnp.concatenate([count] * (width // 128), axis=1)
                if c == 0:
                    value = w[mine * 2 + h, z, part] + t2[0, h, part] + t2[1, h, part]
                else:
                    value = w[4 + z, 2 * h + mine, part] + x2[h, part]
                got[c, us[c], h, vs[c], part] = (value + cfin[c, h, part]) / count
            piece = got.at[c, us[c], :, vs[c], part]
            g_up[c, q] = send(piece, piece, ups[1 - c])
            g_dn[c, q] = send(piece, piece, downs[1 - c])
            h_up[c, q] = send(piece, piece, ups[c])
            h_dn[c, q] = send(piece, piece, downs[c])

    e_up, e_dn = {}, {}

    def spread(c, d):
        piece = got.at[c, us[c], :, v[c][d]]
        e_up[c, d] = send(piece, piece, ups[c])
        e_dn[c, d] = send(piece, piece, downs[c])

    for c in range(2):
        me = us[c]
        g_up[c, 0].wait_recv()
        g_up[c, 1].wait_recv()
        piece = got.at[c, me, 0, v[c][3]]
        f_up[c] = send(piece, piece, ups[1 - c])
        spread(c, 3)
        g_dn[c, 0].wait_recv()
        g_dn[c, 1].wait_recv()
        piece = got.at[c, me, 1, v[c][1]]
        f_dn[c] = send(piece, piece, downs[1 - c])
        spread(c, 1)
    k_up, k_dn = {}, {}

    def onward(c, d):
        b = v[c][d]
        for copy in [h_up[c, 0], h_up[c, 1]] if d == 0 else [e_up[c, d]]:
            copy.wait_recv()
        piece = got.at[c, u[c][3], 0, b]
        k_up[c, d] = send(piece, piece, ups[c])
        for copy in [h_dn[c, 0], h_dn[c, 1]] if d == 0 else [e_dn[c, d]]:
            copy.wait_recv()
        piece = got.at[c, u[c][1], 1, b]
        k_dn[c, d] = send(piece, piece, downs[c])

    for c in range(2):
        onward(c, 0)
    for c in range(2):
        f_up[c].wait_recv()
        f_dn[c].wait_recv()
        spread(c, 2)
    for d in (3, 1, 2):
        for c in range(2):
            onward(c, d)
    for d in (0, 3, 1, 2):
        for c in range(2):
            k_up[c, d].wait_recv()
            k_dn[c, d].wait_recv()
    for copy in sent:
        copy.wait_send()


def store(got, out, sem):
    copies = [
        pltpu.make_async_copy(got.at[c, pl.ds(2 * h, 2)], out.at[c, pl.ds(2 * h, 2)], sem.at[2 * c + h])
        for c in range(2)
        for h in range(2)
    ]
    for copy in copies:
        copy.start()
    for copy in copies:
        copy.wait()


def body(points, centroids):
    n_points, width = points.shape
    n_rows = centroids.shape[0]
    n_cent = lax.axis_size("cent")
    chunk, tile = n_rows // 4, 512
    rows = n_rows // 64
    pieces = (2, 4, 2, 4, rows, width)
    n_copies = 32 + (n_cent - 1) + 1 + 8 + 4 + 4 + 12 + 12 + 2 + 48
    vm = pltpu.VMEM
    flat = (n_rows // chunk, 1, n_points)
    piece = (rows, width)
    lines = (4, 1, 128)
    scratch = [
        vm((n_points, width), BF16),
        vm((n_points, width), BF16),
        vm((8, 4, *piece), F32),
        vm((2, chunk, width), F32),
        vm((n_rows, width), BF16),
        vm((n_rows, 128), F32),
        vm((chunk, tile), F32),
        vm((chunk, tile), F32),
        vm((n_rows, n_points), BF16),
        vm(flat, F32),
        vm(flat, F32),
        vm(flat, F32),
        vm((2, n_points // 128, 128), F32),
        vm((n_cent - 1, 2, n_points // 128, 128), F32),
        vm((2, 1, n_points), F32),
        vm((2, 1, n_points), F32),
        vm((8, 4, *piece), F32),
        vm((2, 4, *piece), F32),
        vm((2, *piece), F32),
        vm((2, 2, *piece), F32),
        vm((2, 2, 2, *piece), F32),
        vm((2, *piece), F32),
        vm((2, 2, *piece), F32),
        vm((2, 2, *piece), F32),
        vm((8, *lines), F32),
        vm((2, *lines), F32),
        vm((2, *lines), F32),
        vm((2, 3, 2, 1, 128), F32),
        pltpu.SemaphoreType.DMA((n_copies,)),
        pltpu.SemaphoreType.DMA((n_copies,)),
        pltpu.SemaphoreType.DMA((10,)),
    ]
    result = pl.pallas_call(
        functools.partial(kernel, n_cent),
        out_shape=pltpu.VMEM(pieces, F32),
        in_specs=[pl.BlockSpec(memory_space=pl.ANY)] * 2,
        out_specs=pl.BlockSpec(memory_space=pltpu.VMEM),
        scratch_shapes=scratch,
        compiler_params=pltpu.CompilerParams(
            collective_id=0, has_side_effects=True, vmem_limit_bytes=54 * 2**20
        ),
    )(points.reshape(8, 4, n_points // 32, width), centroids)
    saved = pl.pallas_call(
        store,
        out_shape=jax.ShapeDtypeStruct(pieces, F32),
        in_specs=[pl.BlockSpec(memory_space=pltpu.VMEM)],
        out_specs=pl.BlockSpec(memory_space=pl.ANY),
        scratch_shapes=[pltpu.SemaphoreType.DMA((4,))],
        compiler_params=pltpu.CompilerParams(vmem_limit_bytes=2**20),
    )(result)
    return saved.reshape(n_rows, width)


def solution(mesh):
    placed = (P("dp", None), P("cent", None))
    return jax.shard_map(
        body, mesh=mesh, in_specs=placed, out_specs=P("cent", None), check_vma=False
    )
```

time: 122 us -> 127 us (1.041)
  Pallas kernels: 122 us -> 126 us
    pallas_call x1, Pallas kernels: 119 us -> 123 us  [body(): pl.pallas_call(functools.partial(kernel, n_cent), out_shape=pltpu.VMEM(pi...]
where the time goes in v4:
time: 127 us
  Pallas kernels  126 us (99%)
    pallas_call x1, Pallas kernels, body(): pl.pallas_call(functools.partial(kernel, n_cent), out_shape=pltpu.VMEM(pi...  123 us
    pallas_call x1, Pallas kernels, body(): pl.pallas_call(store, out_shape=jax.ShapeDtypeStruct(pieces, F32), in_spe...  3.37 us

profile of v4, /device:TPU:0, one launch (start us, length us, event | category | flops | bytes accessed | tf_op | source)
XLA Modules:
  0.0 126.5 jit_solution(2086849119070009909)
XLA Ops:
  0.0 123.0 %shard_map.28.got = f32[2,4,2,4,64,512]{5,4,3,2,1,0:T(8,128)S(1)} custom-call(f32[8,4,64,512]{3,2,1,0:T(8,128)} %bitcast.2, f32[4096,512]{1,0:T(8,128)} %cents.1), custom_call_target="tpu_custom_call" | custom-call | tf_op jit(solution)/shard_map/pallas_call | solution.py:615
  123.0 3.4 %shard_map.29 = f32[2,4,2,4,64,512]{5,4,3,2,1,0:T(8,128)} custom-call(f32[2,4,2,4,64,512]{5,4,3,2,1,0:T(8,128)S(1)} %shard_map.28.got), custom_call_target="tpu_custom_call" | custom-call | tf_op jit(solution)/shard_map/pallas_call | solution.py:625

commit v5 on v2

v5 whole, which is shorter than its diff:
```python
import functools

import jax
import jax.numpy as jnp
from jax import lax
from jax.experimental import pallas as pl
from jax.experimental.pallas import tpu as pltpu
from jax.sharding import PartitionSpec as P

MESH = pl.DeviceIdType.MESH
F32, BF16 = jnp.float32, jnp.bfloat16
LOG2E = 1.4426950408889634


def kernel(
    n_cent,
    points,
    cents,
    got,
    ph,
    cstage,
    ch,
    sqb,
    logit0,
    logit1,
    expo,
    mtop,
    msum,
    factor,
    stat,
    statr,
    row,
    w,
    r1,
    r2,
    t1,
    t2,
    cfin,
    cnt,
    cntx0,
    cntx1,
    cntz,
    ssem,
    rsem,
    lsem,
):
    n_points, width = ph.shape
    chunk = ch.shape[1]
    n_chunk = mtop.shape[0]
    tile = logit0.shape[1]
    n_tile = n_points // tile
    rows = w.shape[4]
    scale = LOG2E / width**0.5

    dp = lax.axis_index("dp")
    ce = lax.axis_index("cent")
    x, z = lax.rem(dp, 4), lax.div(dp, 4)

    def at_x(d):
        return (z * 4 + lax.rem(x + d, 4), ce)

    def at_z(d):
        return (lax.rem(z + d, 4) * 4 + x, ce)

    def at_cent(d):
        return (dp, lax.rem(ce + d, n_cent))

    peers = [at_x(d) for d in (1, 2, 3)] + [at_z(d) for d in (1, 2, 3)]
    peers += [at_cent(d) for d in range(1, n_cent)]
    barrier = pltpu.get_barrier_semaphore()
    for peer in peers:
        pl.semaphore_signal(barrier, inc=1, device_id=peer, device_id_type=MESH)

    used = [0]

    def slots(n):
        used[0] += n
        return used[0] - n

    def remote(i, src, dst, dev, s=0):
        return pltpu.make_async_remote_copy(
            src_ref=src,
            dst_ref=dst,
            send_sem=ssem.at[s],
            recv_sem=rsem.at[i],
            device_id=dev,
            device_id_type=MESH,
        )

    def send(i, src, dst, dev, s=0):
        remote(i, src, dst, dev, s).start()

    def wait(sem, ref):
        pltpu.make_async_copy(ref, ref, sem).wait()

    part = n_points // 4

    def load_points(i):
        return pltpu.make_async_copy(
            points.at[i], w.at[0, i], lsem.at[i]
        )

    def load_cents(i):
        slot = lax.rem(i, 2)
        return pltpu.make_async_copy(
            cents.at[pl.ds(i * chunk, chunk)], cstage.at[slot], lsem.at[4 + slot]
        )

    load_points(0).start()
    load_cents(0).start()
    for i in range(1, 4):
        load_points(i).start()
    load_cents(1).start()

    def round_cents(i):
        slot = lax.rem(i, 2)
        value = cstage[slot]
        ch[slot] = value.astype(BF16)
        sqb[slot] = jnp.broadcast_to(
            jnp.sum(value * value, axis=1, keepdims=True) * scale, (chunk, 128)
        )

    def first(c, t, logit):
        slot = lax.rem(c, 2)
        inner = lax.dot_general(
            ch[slot], ph[t * tile : (t + 1) * tile, :], (((1,), (1,)), ((), ())),
            preferred_element_type=F32,
        )
        value = inner * (2.0 * scale) - jnp.concatenate([sqb[slot]] * (tile // 128), axis=1)
        logit[...] = value
        return jnp.max(value, axis=0, keepdims=True)

    def second(c, t, logit, high):
        at = slice(t * tile, (t + 1) * tile)
        e = jnp.exp2(logit[...] - high)
        base = pl.multiple_of(c * chunk, chunk)
        expo[pl.ds(base, chunk), at] = e.astype(BF16)
        mtop[c, :, at] = high
        msum[c, :, at] = jnp.sum(e, axis=0, keepdims=True)

    logits = (logit0, logit1)

    def on_chunk(c, high, last):
        if not last:
            load_cents(c + 1).wait()

            @pl.when(c + 2 < n_chunk)
            def _():
                load_cents(c + 2).start()

        for t in range(n_tile):
            if t + 1 < n_tile:
                after = first(c, t + 1, logits[(t + 1) % 2])
                if t == 0 and not last:
                    round_cents(c + 1)
            elif not last:
                after = first(c + 1, 0, logits[(t + 1) % 2])
            second(c, t, logits[t % 2], high)
            high = after
        return high

    def round_points(i):
        load_points(i).wait()
        ph[i * part : (i + 1) * part, :] = w[0, i].reshape(part, width).astype(BF16)

    round_points(0)
    load_cents(0).wait()
    round_cents(0)
    high = first(0, 0, logit0)
    for i in range(1, 4):
        round_points(i)
    high = lax.fori_loop(0, n_chunk - 1, lambda c, high: on_chunk(c, high, False), high)
    on_chunk(n_chunk - 1, high, True)

    stats = slots(1)
    top = functools.reduce(jnp.maximum, [mtop[c] for c in range(n_chunk)])
    total = sum(msum[c] * jnp.exp2(mtop[c] - top) for c in range(n_chunk))
    for i in range(n_points // 128):
        stat[0, i : i + 1, :] = top[:, i * 128 : (i + 1) * 128]
        stat[1, i : i + 1, :] = total[:, i * 128 : (i + 1) * 128]
    pl.semaphore_wait(barrier, len(peers))
    for d in range(1, n_cent):
        send(stats, stat, statr.at[d - 1], at_cent(d), 1)

    def absorb():
        wait(rsem.at[stats], statr)
        tops = [stat[0]] + [statr[d, 0] for d in range(n_cent - 1)]
        sums = [stat[1]] + [statr[d, 1] for d in range(n_cent - 1)]
        high = functools.reduce(jnp.maximum, tops)
        inverse = 1.0 / sum(s * jnp.exp2(t - high) for t, s in zip(tops, sums))
        for i in range(n_points // 128):
            row[0, :, i * 128 : (i + 1) * 128] = high[i : i + 1, :]
            row[1, :, i * 128 : (i + 1) * 128] = inverse[i : i + 1, :]
        for c in range(n_chunk):
            factor[c] = jnp.exp2(mtop[c] - row[0]) * row[1]

    us, vs = (x, z), (z, x)
    fins = []
    for c in range(2):
        for h in range(2):
            at = ((c * 4 + us[c]) * 2 + h) * (4 * rows) + vs[c] * rows
            fins.append(
                pltpu.make_async_copy(
                    cents.at[pl.ds(pl.multiple_of(at, rows), rows)],
                    cfin.at[c, h],
                    lsem.at[6 + 2 * c + h],
                )
            )
            fins[-1].start()

    def produce(pieces):
        spots = []
        for block, b in pieces:
            at = block * (4 * rows) + (0 if b is None else b * rows)
            spots.append((pl.multiple_of(at, rows), lax.div(block * (4 * rows), chunk)))
        size = 4 * rows // len(pieces)
        acc = jnp.zeros((4 * rows, width), F32)
        count = jnp.zeros((4 * rows, 128), F32)
        for t in range(n_tile):
            cols = slice(t * tile, (t + 1) * tile)
            parts = [
                (expo[pl.ds(at, size), cols].astype(F32) * factor[group, :, cols]).astype(BF16)
                for at, group in spots
            ]
            resp = parts[0] if len(parts) == 1 else jnp.concatenate(parts, axis=0)
            acc += jnp.dot(resp, ph[cols, :], preferred_element_type=F32)
            wide = resp.astype(F32)
            for l in range(tile // 128):
                count += wide[:, l * 128 : (l + 1) * 128]
        line = jnp.sum(count.T, axis=0, keepdims=True)
        for k in range(4):
            block, b = pieces[k] if len(pieces) == 4 else (pieces[0][0], k)
            w[lax.div(block, 8), lax.rem(lax.div(block, 2), 4), lax.rem(block, 2), b] = acc[
                k * rows : (k + 1) * rows
            ]
            cnt[block, b, :, :rows] = line[:, k * rows : (k + 1) * rows]

    def block_of(c, bu, h):
        return (c * 4 + bu) * 2 + h

    ups = (at_x(1), at_z(1))
    downs = (at_x(3), at_z(3))
    u = [[lax.rem(us[c] + d, 4) for d in range(4)] for c in range(2)]
    v = [[lax.rem(vs[c] + d, 4) for d in range(4)] for c in range(2)]
    order = (2, 1, 3, 0)

    def place(c):
        return x * (1 - c) + z * c, z * (1 - c) + x * c

    def along(c, d):
        return (lax.rem(z + c * d, 4) * 4 + lax.rem(x + (1 - c) * d, 4), ce)

    far, near = slots(8), slots(1)

    def far_copy(c, h, k):
        here, other = place(c)
        step = lax.rem(2 + 3 * k + lax.div(k, 2) * 3 + lax.div(k, 3) * 2, 4)
        b = lax.rem(other + step, 4)
        return remote(
            far + c * 4 + k,
            w.at[c, lax.rem(here + 2, 4), h, b],
            r1.at[c, h, b],
            along(c, 1 + 2 * h),
        )

    def near_copy(c, h):
        here, _ = place(c)
        d = 3 - 2 * h
        return remote(
            near, w.at[c, lax.rem(here + d, 4), h], r2.at[c, 1 - h, h], along(c, d)
        )

    def farthest(k, carry):
        step = lax.rem(2 + 3 * k + lax.div(k, 2) * 3 + lax.div(k, 3) * 2, 4)
        produce(
            [
                (block_of(c, lax.rem(place(c)[0] + 2, 4), h), lax.rem(place(c)[1] + step, 4))
                for h in range(2)
                for c in range(2)
            ]
        )
        for h in range(2):
            for c in range(2):
                far_copy(c, h, k).start()
        return carry

    def nearest(i, carry):
        c, h = lax.rem(i, 2), 1 - lax.div(i, 2)
        produce([(block_of(c, lax.rem(place(c)[0] + 3 - 2 * h, 4), h), None)])
        near_copy(c, h).start()
        return carry

    def others(i, carry):
        c, h, mine = lax.rem(i, 2), lax.rem(lax.div(i, 2), 2), lax.div(i, 4)
        produce([(block_of(c, lax.rem(place(c)[0] + (1 - mine) * (1 + 2 * h), 4), h), None)])
        return carry

    absorb()
    lax.fori_loop(0, 4, farthest, 0)
    lax.fori_loop(0, 4, nearest, 0)
    lax.fori_loop(0, 8, others, 0)
    xrec = slots(2)
    for d in (1, 2, 3):
        to = lax.rem(x + d, 4)
        send(xrec, cnt.at[pl.ds(2 * to, 2)], cntx0.at[d - 1], at_x(d), 2)
        send(xrec + 1, cnt.at[pl.ds(8, 8), to], cntx1.at[d - 1], at_x(d), 3)

    two, four = w.at[0, 0, 0, pl.ds(0, 2)], w.at[0, 0, 0]
    tail = slots(8)
    for k, d in enumerate(order):
        for c in range(2):
            b = v[c][d]
            wait(rsem.at[far + c * 4 + k], two)
            at = tail + c * 4 + k
            w[c, u[c][1], 0, b] += r1[c, 0, b]
            send(at, w.at[c, u[c][1], 0, b], r2.at[c, 0, 0, b], ups[c])
            w[c, u[c][3], 1, b] += r1[c, 1, b]
            send(at, w.at[c, u[c][3], 1, b], r2.at[c, 1, 1, b], downs[c])
    wait(rsem.at[xrec], cntx0)
    wait(rsem.at[xrec + 1], cntx1)
    mine = pl.ds(2 * x, 2)
    cnt[mine] = cnt[mine] + cntx0[0] + cntx0[1] + cntx0[2]
    cnt[8:16, x] = cnt[8:16, x] + cntx1[0] + cntx1[1] + cntx1[2]
    zrec = slots(1)
    for d in (1, 2, 3):
        to = lax.rem(z + d, 4)
        send(zrec, cnt.at[mine, to], cntz.at[0, d - 1], at_z(d), 4)
        send(zrec, cnt.at[pl.ds(8 + 2 * to, 2), x], cntz.at[1, d - 1], at_z(d), 4)
    wait(rsem.at[near], w.at[0, pl.ds(0, 2)])

    ups2, downs2 = ups[::-1], downs[::-1]
    halves = [pl.ds(q * (rows // 2), rows // 2) for q in range(2)]
    early, ends = slots(4), slots(2)

    def pass_on(c, h, d, q):
        side = h if d is None else 1 - h
        to = (ups2, downs2)[side][c]
        b = v[c][d or (1 + 2 * h)]
        send(
            ends + q, w.at[c, us[c], h, b, halves[q]], t2.at[c, side, h, halves[q]], to
        )

    for k, d in enumerate(order):
        for c in range(2):
            b, me = v[c][d], us[c]
            wait(rsem.at[tail + c * 4 + k], two)
            for h in range(2):
                w[c, me, h, b] += r2[c, 0, h, b] + r2[c, 1, h, b]
            if d == 2:
                for q in range(2):
                    part, at = halves[q], early + 2 * c + q
                    send(at, w.at[c, me, 0, b, part], t1.at[c, 0, part], ups2[c])
                    send(at, w.at[c, me, 1, b, part], t1.at[c, 1, part], downs2[c])
            if d == 1:
                pass_on(c, 1, 1, 0)
            if d == 3:
                pass_on(c, 0, 3, 0)
    for q in range(2):
        if q == 1:
            for c in range(2):
                pass_on(c, 1, 1, 1)
                pass_on(c, 0, 3, 1)
        for c in range(2):
            me, part = us[c], halves[q]
            wait(rsem.at[early + 2 * c + q], w.at[0, 0, 0, 0])
            w[c, me, 0, v[c][1], part] += t1[c, 0, part]
            pass_on(c, 0, None, q)
            w[c, me, 1, v[c][3], part] += t1[c, 1, part]
            pass_on(c, 1, None, q)

    wait(rsem.at[zrec], cntz)
    for copy in fins:
        copy.wait()
    counts = {}
    for c in range(2):
        for h in range(2):
            line = cnt[(c * 4 + us[c]) * 2 + h, vs[c]]
            line = line + cntz[c, 0, h] + cntz[c, 1, h] + cntz[c, 2, h]
            counts[c, h] = jnp.broadcast_to(line, (128, 128)).T + 1.0
    g, h_, f, e, k_ = slots(4), slots(2), slots(2), slots(6), slots(1)
    for q in range(2):
        wait(rsem.at[ends + q], four)
        part = halves[q]
        for c in range(2):
            me, b = us[c], vs[c]
            for h in range(2):
                count = counts[c, h][q * (rows // 2) : (q + 1) * (rows // 2)]
                count = jnp.concatenate([count] * (width // 128), axis=1)
                value = w[c, me, h, b, part] + t2[c, 0, h, part] + t2[c, 1, h, part]
                got[c, me, h, b, part] = (value + cfin[c, h, part]) / count
            piece = got.at[c, me, :, b, part]
            send(g + 2 * c, piece, piece, ups2[c])
            send(g + 2 * c + 1, piece, piece, downs2[c])
        for c in range(2):
            piece = got.at[c, us[c], :, vs[c], part]
            send(h_ + c, piece, piece, ups[c])
            send(h_ + c, piece, piece, downs[c])

    def spread(c, d):
        piece = got.at[c, us[c], :, v[c][d]]
        at = e + 3 * c + d - 1
        send(at, piece, piece, ups[c])
        send(at, piece, piece, downs[c])

    def onward(c, d):
        b = v[c][d]
        wait(rsem.at[h_ + c if d == 0 else e + 3 * c + d - 1], four)
        piece = got.at[c, u[c][3], 0, b]
        send(k_, piece, piece, ups[c])
        piece = got.at[c, u[c][1], 1, b]
        send(k_, piece, piece, downs[c])

    for c in range(2):
        wait(rsem.at[g + 2 * c], two)
        piece = got.at[c, us[c], 0, v[c][3]]
        send(f + c, piece, piece, ups2[c])
        spread(c, 3)
        wait(rsem.at[g + 2 * c + 1], two)
        piece = got.at[c, us[c], 1, v[c][1]]
        send(f + c, piece, piece, downs2[c])
        spread(c, 1)
    for c in range(2):
        onward(c, 0)
    for c in range(2):
        wait(rsem.at[f + c], two)
        spread(c, 2)
    for d in (3, 1, 2):
        for c in range(2):
            onward(c, d)
    wait(rsem.at[k_], w.at[0, pl.ds(0, 2)])
    total_rows = expo.shape[0] * 15 // 16
    wait(ssem.at[0], expo.at[pl.ds(0, total_rows)])
    wait(ssem.at[1], statr)
    wait(ssem.at[2], cntx0)
    wait(ssem.at[3], cntx1)
    wait(ssem.at[4], cntz)


def store(got, out, sem):
    copies = [
        pltpu.make_async_copy(got.at[c, pl.ds(2 * h, 2)], out.at[c, pl.ds(2 * h, 2)], sem.at[2 * c + h])
        for c in range(2)
        for h in range(2)
    ]
    for copy in copies:
        copy.start()
    for copy in copies:
        copy.wait()


def body(points, centroids):
    n_points, width = points.shape
    n_rows = centroids.shape[0]
    n_cent = lax.axis_size("cent")
    chunk, tile = n_rows // 4, 512
    rows = n_rows // 64
    pieces = (2, 4, 2, 4, rows, width)
    n_groups = 1 + 9 + 2 + 8 + 1 + 6 + 15
    vm = pltpu.VMEM
    flat = (n_rows // chunk, 1, n_points)
    scratch = [
        vm((n_points, width), BF16),
        vm((2, chunk, width), F32),
        vm((2, chunk, width), BF16),
        vm((2, chunk, 128), F32),
        vm((chunk, tile), F32),
        vm((chunk, tile), F32),
        vm((n_rows, n_points), BF16),
        vm(flat, F32),
        vm(flat, F32),
        vm(flat, F32),
        vm((2, n_points // 128, 128), F32),
        vm((n_cent - 1, 2, n_points // 128, 128), F32),
        vm((2, 1, n_points), F32),
        vm(pieces, F32),
        vm((2, 2, 4, rows, width), F32),
        vm((2, 2, 2, 4, rows, width), F32),
        vm((2, 2, rows, width), F32),
        vm((2, 2, 2, rows, width), F32),
        vm((2, 2, rows, width), F32),
        vm((16, 4, 1, 128), F32),
        vm((3, 2, 4, 1, 128), F32),
        vm((3, 8, 1, 128), F32),
        vm((2, 3, 2, 1, 128), F32),
        pltpu.SemaphoreType.DMA((5,)),
        pltpu.SemaphoreType.DMA((n_groups,)),
        pltpu.SemaphoreType.DMA((10,)),
    ]
    result = pl.pallas_call(
        functools.partial(kernel, n_cent),
        out_shape=pltpu.VMEM(pieces, F32),
        in_specs=[pl.BlockSpec(memory_space=pl.ANY)] * 2,
        out_specs=pl.BlockSpec(memory_space=pltpu.VMEM),
        scratch_shapes=scratch,
        compiler_params=pltpu.CompilerParams(
            collective_id=0, has_side_effects=True, vmem_limit_bytes=54 * 2**20
        ),
    )(points.reshape(4, 2, 4, n_points // 32, width), centroids)
    saved = pl.pallas_call(
        store,
        out_shape=jax.ShapeDtypeStruct(pieces, F32),
        in_specs=[pl.BlockSpec(memory_space=pltpu.VMEM)],
        out_specs=pl.BlockSpec(memory_space=pl.ANY),
        scratch_shapes=[pltpu.SemaphoreType.DMA((4,))],
        compiler_params=pltpu.CompilerParams(vmem_limit_bytes=2**20),
    )(result)
    return saved.reshape(n_rows, width)


def solution(mesh):
    placed = (P("dp", None), P("cent", None))
    return jax.shard_map(
        body, mesh=mesh, in_specs=placed, out_specs=P("cent", None), check_vma=False
    )
```

time: 122 us -> 116 us (0.951)
  Pallas kernels: 122 us -> 115 us
    pallas_call x1, Pallas kernels: 119 us -> 112 us  [body(): pl.pallas_call(functools.partial(kernel, n_cent), out_shape=pltpu.VMEM(pi...]
where the time goes in v5:
time: 116 us; the launch traced here: 115 us
  Pallas kernels  115 us (99%)
    pallas_call x1, Pallas kernels, body(): pl.pallas_call(functools.partial(kernel, n_cent), out_shape=pltpu.VMEM(pi...  112 us
    pallas_call x1, Pallas kernels, body(): pl.pallas_call(store, out_shape=jax.ShapeDtypeStruct(pieces, F32), in_spe...  3.37 us

profile of v5, /device:TPU:0, one launch (start us, length us, event | category | flops | bytes accessed | tf_op | source)
XLA Modules:
  0.0 115.4 jit_solution(10683830104227179324)
XLA Ops:
  0.0 112.1 %shard_map.28.got = f32[2,4,2,4,64,512]{5,4,3,2,1,0:T(8,128)S(1)} custom-call(f32[4,2,4,64,512]{4,3,2,1,0:T(8,128)} %bitcast.2, f32[4096,512]{1,0:T(8,128)} %cents.1), custom_call_target="tpu_custom_call" | custom-call | tf_op jit(solution)/shard_map/pallas_call | solution.py:489
  112.1 3.4 %shard_map.29 = f32[2,4,2,4,64,512]{5,4,3,2,1,0:T(8,128)} custom-call(f32[2,4,2,4,64,512]{5,4,3,2,1,0:T(8,128)S(1)} %shard_map.28.got), custom_call_target="tpu_custom_call" | custom-call | tf_op jit(solution)/shard_map/pallas_call | solution.py:499

commit v6 on v5

--- a/solution.py
+++ b/solution.py
@@ -18,6 +18,7 @@
     cents,
     got,
     ph,
+    pt,
     cstage,
     ch,
     sqb,
@@ -123,7 +124,7 @@
     def first(c, t, logit):
         slot = lax.rem(c, 2)
         inner = lax.dot_general(
-            ch[slot], ph[t * tile : (t + 1) * tile, :], (((1,), (1,)), ((), ())),
+            ch[slot], pt[:, t * tile : (t + 1) * tile], (((1,), (0,)), ((), ())),
             preferred_element_type=F32,
         )
         value = inner * (2.0 * scale) - jnp.concatenate([sqb[slot]] * (tile // 128), axis=1)
@@ -161,7 +162,9 @@
 
     def round_points(i):
         load_points(i).wait()
-        ph[i * part : (i + 1) * part, :] = w[0, i].reshape(part, width).astype(BF16)
+        half = w[0, i].reshape(part, width).astype(BF16)
+        ph[i * part : (i + 1) * part, :] = half
+        pt[:, i * part : (i + 1) * part] = half.T
 
     round_points(0)
     load_cents(0).wait()
@@ -460,6 +463,7 @@
     flat = (n_rows // chunk, 1, n_points)
     scratch = [
         vm((n_points, width), BF16),
+        vm((width, n_points), BF16),
         vm((2, chunk, width), F32),
         vm((2, chunk, width), BF16),
         vm((2, chunk, 128), F32),
@@ -493,7 +497,7 @@
         out_specs=pl.BlockSpec(memory_space=pltpu.VMEM),
         scratch_shapes=scratch,
         compiler_params=pltpu.CompilerParams(
-            collective_id=0, has_side_effects=True, vmem_limit_bytes=54 * 2**20
+            collective_id=0, has_side_effects=True, vmem_limit_bytes=55 * 2**20
         ),
     )(points.reshape(4, 2, 4, n_points // 32, width), centroids)
     saved = pl.pallas_call(

time: 116 us -> 115 us (level)
  no operation moved by 1% of the time
where the time goes in v6:
time: 115 us
  Pallas kernels  115 us (100%)
    pallas_call x1, Pallas kernels, body(): pl.pallas_call(functools.partial(kernel, n_cent), out_shape=pltpu.VMEM(pi...  112 us
    pallas_call x1, Pallas kernels, body(): pl.pallas_call(store, out_shape=jax.ShapeDtypeStruct(pieces, F32), in_spe...  3.37 us

profile of v6, /device:TPU:0, one launch (start us, length us, event | category | flops | bytes accessed | tf_op | source)
XLA Modules:
  0.0 115.3 jit_solution(10008470366052027478)
XLA Ops:
  0.0 111.9 %shard_map.28.got = f32[2,4,2,4,64,512]{5,4,3,2,1,0:T(8,128)S(1)} custom-call(f32[4,2,4,64,512]{4,3,2,1,0:T(8,128)} %bitcast.2, f32[4096,512]{1,0:T(8,128)} %cents.1), custom_call_target="tpu_custom_call" | custom-call | tf_op jit(solution)/shard_map/pallas_call | solution.py:493
  111.9 3.4 %shard_map.29 = f32[2,4,2,4,64,512]{5,4,3,2,1,0:T(8,128)} custom-call(f32[2,4,2,4,64,512]{5,4,3,2,1,0:T(8,128)S(1)} %shard_map.28.got), custom_call_target="tpu_custom_call" | custom-call | tf_op jit(solution)/shard_map/pallas_call | solution.py:503

commit v7 on v6

--- a/solution.py
+++ b/solution.py
@@ -455,7 +455,7 @@
     n_points, width = points.shape
     n_rows = centroids.shape[0]
     n_cent = lax.axis_size("cent")
-    chunk, tile = n_rows // 4, 512
+    chunk, tile = n_rows // 8, 512
     rows = n_rows // 64
     pieces = (2, 4, 2, 4, rows, width)
     n_groups = 1 + 9 + 2 + 8 + 1 + 6 + 15
@@ -497,7 +497,7 @@
         out_specs=pl.BlockSpec(memory_space=pltpu.VMEM),
         scratch_shapes=scratch,
         compiler_params=pltpu.CompilerParams(
-            collective_id=0, has_side_effects=True, vmem_limit_bytes=55 * 2**20
+            collective_id=0, has_side_effects=True, vmem_limit_bytes=54 * 2**20
         ),
     )(points.reshape(4, 2, 4, n_points // 32, width), centroids)
     saved = pl.pallas_call(

time: 115 us -> 115 us (level)
  no operation moved by 1% of the time
where the time goes in v7:
time: 115 us
  Pallas kernels  115 us (100%)
    pallas_call x1, Pallas kernels, body(): pl.pallas_call(functools.partial(kernel, n_cent), out_shape=pltpu.VMEM(pi...  112 us
    pallas_call x1, Pallas kernels, body(): pl.pallas_call(store, out_shape=jax.ShapeDtypeStruct(pieces, F32), in_spe...  3.37 us

profile of v7, /device:TPU:0, one launch (start us, length us, event | category | flops | bytes accessed | tf_op | source)
XLA Modules:
  0.0 115.0 jit_solution(16800918394427347218)
XLA Ops:
  0.0 111.6 %shard_map.28.got = f32[2,4,2,4,64,512]{5,4,3,2,1,0:T(8,128)S(1)} custom-call(f32[4,2,4,64,512]{4,3,2,1,0:T(8,128)} %bitcast.2, f32[4096,512]{1,0:T(8,128)} %cents.1), custom_call_target="tpu_custom_call" | custom-call | tf_op jit(solution)/shard_map/pallas_call | solution.py:493
  111.6 3.4 %shard_map.29 = f32[2,4,2,4,64,512]{5,4,3,2,1,0:T(8,128)} custom-call(f32[2,4,2,4,64,512]{5,4,3,2,1,0:T(8,128)S(1)} %shard_map.28.got), custom_call_target="tpu_custom_call" | custom-call | tf_op jit(solution)/shard_map/pallas_call | solution.py:503
